TPU v7x, 256 devices: a whole 4x4x8 slice. The times are simulated.
256 devices in a mesh: gz: 64 (over z, x, core), col: 4 (over y).
Axes of the slice: x: 4, y: 4, z: 8, core: 2. Of those that a mesh axis runs over, the one named last changes fastest.
Arguments:
- source: float32 [4096, 2048], P('gz', 'col'), may hold values from -6 to 6
- z_vectors: float32 [4096, 4096], P('gz', 'col'), may hold values from -0.25 to 0.25
- x_vectors: float32 [4, 4], replicated, may hold values from -3 to 3
- y_vectors: float32 [512, 512], replicated, may hold values from -0.25 to 0.25
- z_values: float32 [4096], replicated, may hold values from 0.1 to 3
- x_values: float32 [4], replicated, may hold values from 0.1 to 3
- y_values: float32 [512], replicated, may hold values from 0.1 to 3
Outputs:
- solution: float32 [4096, 2048], P('gz', 'col')
All inputs are finite; a program needn't handle non-finite values.
Results may differ from a plain program's by a relative error of at most 0.000092.
Values sent between devices are 32-bit elements; how exact they have to be, the bound alone decides.
No kernel may reach another device: no remote copies, remote signals or barrier semaphores. Data moves between devices by JAX's collectives and lax.ppermute only.
A program may use at most 64 MiB of HBM per device.

v0:
```python
import functools
import jax
import jax.numpy as jnp
from jax import lax
from jax.experimental import pallas as pl
from jax.experimental.pallas import tpu as pltpu
from jax.sharding import Mesh
from jax.sharding import PartitionSpec as P

NZ_CHIPS, NX_CHIPS, CORES, NY_CHIPS = 8, 4, 2, 4
GZ = ("z", "x", "core")
SIZE = {"z": NZ_CHIPS, "x": NX_CHIPS, "core": CORES, "y": NY_CHIPS}
OFFSETS = (4, 0, -1, -2, -3, 1, 2, 3)


VMEM = pl.BlockSpec(memory_space=pltpu.VMEM)
SMEM = pl.BlockSpec(memory_space=pltpu.SMEM)


def f32(*shape):
    return jax.ShapeDtypeStruct(shape, jnp.float32)


def bf16(*shape):
    return jax.ShapeDtypeStruct(shape, jnp.bfloat16)


def shifted(value, axis, step):
    n = SIZE[axis]
    return lax.ppermute(value, axis, [(i, (i + step) % n) for i in range(n)])


def two_parts(value):
    high = value.astype(jnp.bfloat16)
    return high, (value - high.astype(jnp.float32)).astype(jnp.bfloat16)


def product(left, right, dims):
    one = functools.partial(
        lax.dot_general, dimension_numbers=(dims, ((), ())), preferred_element_type=jnp.float32
    )
    (lh, ll), (rh, rl) = left, right
    return one(lh, rh) + (one(ll, rh) + one(lh, rl))


NN = ((1,), (0,))
NT = ((1,), (1,))


def left_lanes(like):
    return lax.broadcasted_iota(jnp.int32, like.shape, 1) < 64


def swapped_in(a, b):
    left = left_lanes(a)
    return jnp.where(left, a, pltpu.roll(b, 64, 1)), jnp.where(left, pltpu.roll(a, 64, 1), b)


def place(axis, step=0):
    return lax.rem(lax.axis_index(axis) + (2 * SIZE[axis] + step), SIZE[axis])


def mixed(weights, parts):
    total = None
    for weight, part in zip(weights, parts):
        total = weight * part if total is None else total + weight * part
    return total


def along_y_kernel(source, y_vectors, packed, y_high, y_low, rows, vectors, sems):
    copies = [pltpu.make_async_copy(source, rows, sems.at[0])]
    for part in range(4):
        piece = pl.ds(128 * part, 128)
        copies.append(pltpu.make_async_copy(y_vectors.at[piece], vectors.at[piece], sems.at[part + 1]))
    for copy in copies:
        copy.start()
    copies[0].wait()
    high, low = two_parts(rows[...])
    along_y = None
    for part in range(4):
        piece = slice(128 * part, 128 * part + 128)
        copies[part + 1].wait()
        y_high[piece], y_low[piece] = two_parts(vectors[piece])
        term = product((high[:, piece], low[:, piece]), (y_high[piece], y_low[piece]), NN)
        along_y = term if along_y is None else along_y + term
    for g in range(NZ_CHIPS // 2):
        lanes = slice(128 * g, 128 * g + 128)
        even, odd = swapped_in(along_y[:32, lanes], along_y[32:, lanes])
        packed[2 * g] = even
        packed[2 * g + 1] = odd


def divisor_kernel(x_values, z_values, y_values, out, column):
    z = lax.axis_index("z")
    row = lax.axis_index("y") * 8 + lax.axis_index("core") * 4 + lax.axis_index("x")
    of_z = z_values[pl.ds(row, 1), :]
    of_y = y_values[pl.ds(lax.div(z, 2), 1), :]
    column[...] = jnp.broadcast_to(of_y, (128, 128)).T
    of_y = column[pl.ds(pl.multiple_of(lax.rem(z, 2) * 64, 64), 64), :]
    for i in range(4):
        out[64 * i : 64 * i + 64] = (of_z + x_values[i]) + of_y


def half_kernel(first, came, out):
    out[...] = came[first : first + 32]


def forward_kernel(x_vectors, *refs):
    zs, planes, (partial, z_high, z_low, far_high, far_low), (field,) = (
        refs[:7], refs[7:11], refs[11:16], refs[16:]
    )
    z_high[:64] = jnp.zeros((64, 1024), jnp.bfloat16)
    z_low[:64] = jnp.zeros((64, 1024), jnp.bfloat16)
    weights = [[x_vectors[place("y", -s), i] for s in range(4)] for i in range(4)]
    for p, offset in enumerate(OFFSETS):
        rows = slice(64 * p, 64 * p + 64)
        if p:
            z_high[rows], z_low[rows] = two_parts(zs[p - 1][...])
        block = place("z", offset)
        mine = [plane[block] for plane in planes]
        modes = [mixed(weights[i], mine) for i in range(4)]
        for pair in range(2):
            top, bottom = swapped_in(modes[2 * pair], modes[2 * pair + 1])
            lanes = slice(128 * pair, 128 * pair + 128)
            field[64 * p : 64 * p + 32, lanes] = top
            field[64 * p + 32 : 64 * p + 64, lanes] = bottom
    high, low = two_parts(field[...].T)
    far_high[...], far_low[...] = high[:, :128], low[:, :128]
    for tile in range(4):
        lanes = slice(256 * tile, 256 * tile + 256)
        partial[:, lanes] = product((high, low), (z_high[:, lanes], z_low[:, lanes]), NN)


def forward_far_kernel(partial, field_high, field_low, top, bottom, to_partner, kept, far_high, far_low):
    core = lax.axis_index("core")
    far_high[:32], far_low[:32] = two_parts(top[...])
    far_high[32:], far_low[32:] = two_parts(bottom[...])
    field = field_high[:, :64], field_low[:, :64]
    for out, half in ((to_partner, 1 - core), (kept, core)):
        for tile in range(2):
            lanes = pl.ds(pl.multiple_of(half * 512 + tile * 256, 256), 256)
            out[:, 256 * tile : 256 * tile + 256] = partial[:, lanes] + product(
                field, (far_high[:, lanes], far_low[:, lanes]), NN
            )


def by_owner_kernel(kept, received, *outs):
    for s, out in enumerate(outs):
        lanes = pl.ds(pl.multiple_of(place("x", s) * 128, 128), 128)
        out[...] = kept[:, lanes] + received[:, lanes]


def scaled_kernel(a, b, c, d, divisor, out):
    out[...] = ((a[...] + b[...]) + (c[...] + d[...])) / divisor[...]


def backward_kernel(x_vectors, z_high, z_low, far_high, far_low, *refs):
    blocks, outs, (s_high, s_low, first_high, first_low) = refs[:8], refs[8:12], refs[12:]
    for first, far, whole in ((first_high, far_high, z_high), (first_low, far_low, z_low)):
        first[:64] = far[...]
        first[64:] = whole[64:256]
    core = lax.axis_index("core")
    for number, block in enumerate(blocks):
        half = core if number < 4 else 1 - core
        lanes = pl.ds(pl.multiple_of(half * 512 + place("x", -number) * 128, 128), 128)
        s_high[:, lanes], s_low[:, lanes] = two_parts(block[...])
    modes = s_high[...], s_low[...]
    weights = [[x_vectors[place("y", s), i] for i in range(4)] for s in range(4)]
    for p in range(8):
        at = 64 * (p % 4)
        if p == 0:
            part = product((first_high[...], first_low[...]), modes, NT)
        elif p == 4:
            part = product((z_high[256:], z_low[256:]), modes, NT)
        packed = []
        for pair in range(2):
            lanes = slice(128 * pair, 128 * pair + 128)
            packed += swapped_in(part[at : at + 32, lanes], part[at + 32 : at + 64, lanes])
        block = place("z", OFFSETS[p])
        for s, out in enumerate(outs):
            out[block] = mixed(weights[s], packed)


def along_y_back_kernel(packed, y_high, y_low, out, field):
    for g in range(NZ_CHIPS // 2):
        lanes = slice(128 * g, 128 * g + 128)
        field[:32, lanes], field[32:, lanes] = swapped_in(packed[2 * g], packed[2 * g + 1])
    out[...] = product(two_parts(field[...]), (y_high[...], y_low[...]), NT)


def call(kernel, out_shape, operands, smem=0, scratch=(), flops=0, vmem=16 << 20, held=VMEM):
    outs = out_shape if isinstance(out_shape, (tuple, list)) else (out_shape,)
    moved = sum(a.size * a.dtype.itemsize for a in (*operands, *outs))
    return pl.pallas_call(
        kernel,
        out_shape=out_shape,
        in_specs=[SMEM] * smem + [held] * (len(operands) - smem),
        out_specs=VMEM if outs is not out_shape else [VMEM] * len(outs),
        scratch_shapes=list(scratch),
        cost_estimate=pl.CostEstimate(flops=flops, bytes_accessed=moved, transcendentals=0),
        compiler_params=pltpu.CompilerParams(vmem_limit_bytes=vmem),
    )(*operands)


def shards(source, z_vectors, x_vectors, y_vectors, z_values, x_values, y_values):
    packed, y_high, y_low = call(
        along_y_kernel,
        (f32(8, 32, 128), bf16(512, 512), bf16(512, 512)),
        (source, y_vectors),
        flops=2 * 64 * 512 * 512 * 3,
        scratch=[
            pltpu.VMEM((64, 512), jnp.float32),
            pltpu.VMEM((512, 512), jnp.float32),
            pltpu.SemaphoreType.DMA((5,)),
        ],
        held=pl.BlockSpec(memory_space=pltpu.HBM),
        vmem=60 << 20,
    )
    right1 = shifted(z_vectors, "z", 1)
    left1 = shifted(z_vectors, "z", -1)
    plane = lax.all_to_all(packed, "z", 0, 0, tiled=True)
    divisor = call(
        divisor_kernel,
        f32(256, 128),
        (x_values, z_values.reshape(32, 128), y_values.reshape(4, 128)),
        smem=1,
        scratch=[pltpu.VMEM((128, 128), jnp.float32)],
    )
    right2, left2 = shifted(right1, "z", 1), shifted(left1, "z", -1)
    planes = [plane] + [shifted(plane, "y", s) for s in (1, 2, 3)]
    right3, left3 = shifted(right2, "z", 1), shifted(left2, "z", -1)
    top = call(functools.partial(half_kernel, 0), f32(32, 1024), (right3,), vmem=1 << 20)
    bottom = call(functools.partial(half_kernel, 32), f32(32, 1024), (left3,), vmem=1 << 20)
    top, bottom = shifted(top, "z", 1), shifted(bottom, "z", -1)

    partial, z_high, z_low, field_high, field_low = call(
        forward_kernel,
        (f32(256, 1024), bf16(512, 1024), bf16(512, 1024), bf16(256, 128), bf16(256, 128)),
        (x_vectors, z_vectors, right1, right2, right3, left1, left2, left3, *planes),
        smem=1,
        scratch=[pltpu.VMEM((512, 256), jnp.float32)],
        flops=2 * 512 * 256 * 1024 * 3,
    )
    to_partner, kept, far_high, far_low = call(
        forward_far_kernel,
        (f32(256, 512), f32(256, 512), bf16(64, 1024), bf16(64, 1024)),
        (partial, field_high, field_low, top, bottom),
        flops=2 * 64 * 256 * 1024 * 3,
    )
    received = shifted(to_partner, "core", 1)
    mine, *others = call(by_owner_kernel, (f32(256, 128),) * 4, (kept, received))
    sums = [shifted(part, "x", s) for s, part in enumerate(others, 1)]
    scaled = call(scaled_kernel, f32(256, 128), (mine, *sums, divisor))

    modes = [scaled] + [shifted(scaled, "x", s) for s in (1, 2, 3)]
    across = [shifted(block, "core", 1) for block in modes]
    z_parts = z_high, z_low, far_high, far_low
    mine, *others = call(
        backward_kernel,
        (f32(8, 32, 128),) * 4,
        (x_vectors, *z_parts, *modes, *across),
        smem=1,
        scratch=[pltpu.VMEM((256, 1024), jnp.bfloat16)] * 4,
        flops=2 * 512 * 256 * 1024 * 3,
    )
    for s, part in enumerate(others, 1):
        mine = mine + shifted(part, "y", s)
    back = lax.all_to_all(mine, "z", 0, 0, tiled=True)
    return call(
        along_y_back_kernel,
        f32(64, 512),
        (back, y_high, y_low),
        scratch=[pltpu.VMEM((64, 512), jnp.float32)],
        flops=2 * 64 * 512 * 512 * 3,
    )


def solution(mesh):
    devices = mesh.devices.reshape(NZ_CHIPS, NX_CHIPS, CORES, NY_CHIPS)
    torus = Mesh(devices, ("z", "x", "core", "y"))

    return jax.shard_map(
        shards,
        mesh=torus,
        in_specs=(P(GZ, "y"), P(GZ, "y"), P(), P(), P(), P(), P()),
        out_specs=P(GZ, "y"),
        check_vma=False,
    )
```

profile of v0, /device:TPU:1, one launch (start us, length us, event | category | flops | bytes accessed | tf_op | source)
XLA Modules:
  0.0 94.5 jit_solution(4567518798024051836)
XLA Ops:
  0.0 6.4 %collective-permute-start.3 = (f32[64,1024]{1,0:T(8,128)}, f32[64,1024]{1,0:T(8,128)S(1)}, u32[]{:S(2)}, u32[]{:S(2)}) collective-permute-start(f32[64,1024]{1,0:T(8,128)} %refs_0_.1), channel_id=1, source_target_pairs={{0,224},{32,0},{64,32},{96,64},{128,96},{160,128},{192,160},{224,1... | collective-permute-start | bytes 786440 | tf_op jit(solution)/shard_map/ppermute | solution.py:30
  6.4 0.0 collective-permute-start
  6.4 5.3 %collective-permute-done.3.refs_4_ = f32[64,1024]{1,0:T(8,128)S(1)} collective-permute-done((f32[64,1024]{1,0:T(8,128)}, f32[64,1024]{1,0:T(8,128)S(1)}, u32[]{:S(2)}, u32[]{:S(2)}) %collective-permute-start.3) | collective-permute-done | bytes 262176 | tf_op jit(solution)/shard_map/ppermute | solution.py:30
  11.7 3.3 %collective-permute-start.4 = (f32[64,1024]{1,0:T(8,128)S(1)}, f32[64,1024]{1,0:T(8,128)S(1)}, u32[]{:S(2)}, u32[]{:S(2)}) collective-permute-start(f32[64,1024]{1,0:T(8,128)S(1)} %collective-permute-done.3.refs_4_), channel_id=1, source_target_pairs={{0,224},{32,0},{64,32},{96,64},{128,96},{160,128},{192,160},{224,1... | collective-permute-start | bytes 786440 | tf_op jit(solution)/shard_map/ppermute | solution.py:30
  15.0 2.4 %shard_map.73 = (f32[8,32,128]{2,1,0:T(8,128)}, bf16[512,512]{1,0:T(8,128)(2,1)}, bf16[512,512]{1,0:T(8,128)(2,1)}) custom-call(f32[64,512]{1,0:T(8,128)} %source.1, f32[512,512]{1,0:T(8,128)} %y_vectors.1), custom_call_target="tpu_custom_call" | custom-call | flops 100663296 | bytes 2359296 | tf_op jit(solution)/shard_map/pallas_call | solution.py:194
  17.4 4.0 %all-to-all-start = ((f32[8,32,128]{2,1,0:T(8,128)}), f32[8,32,128]{2,1,0:T(8,128)S(1)}, u32[]{:S(2)}, u32[]{:S(2)}) async-start(f32[8,32,128]{2,1,0:T(8,128)} %get-tuple-element.25), calls=%async_computation | async-start | bytes 262144 | tf_op jit(solution)/shard_map/all_to_all | solution.py:221
  21.4 2.7 %collective-permute-start.5 = (f32[64,1024]{1,0:T(8,128)S(1)}, f32[64,1024]{1,0:T(8,128)S(1)}, u32[]{:S(2)}, u32[]{:S(2)}) collective-permute-start(f32[64,1024]{1,0:T(8,128)S(1)} %collective-permute-done.4.refs_5_), channel_id=1, source_target_pairs={{0,224},{32,0},{64,32},{96,64},{128,96},{160,128},{192,160},{224,1... | collective-permute-start | bytes 786440 | tf_op jit(solution)/shard_map/ppermute | solution.py:30
  24.1 5.4 %all-to-all-done.refs_7_ = f32[8,32,128]{2,1,0:T(8,128)S(1)} async-done(((f32[8,32,128]{2,1,0:T(8,128)}), f32[8,32,128]{2,1,0:T(8,128)S(1)}, u32[]{:S(2)}, u32[]{:S(2)}) %all-to-all-start) | async-done | bytes 131104 | tf_op jit(solution)/shard_map/all_to_all | solution.py:221
  29.5 1.3 %collective-permute-start.6 = (f32[8,32,128]{2,1,0:T(8,128)S(1)}, f32[8,32,128]{2,1,0:T(8,128)S(1)}, u32[]{:S(2)}, u32[]{:S(2)}) collective-permute-start(f32[8,32,128]{2,1,0:T(8,128)S(1)} %all-to-all-done.refs_7_), channel_id=1, source_target_pairs={{0,1},{1,2},{2,3},{3,0},{4,5},{5,6},{6,7},{7,4},{8,9},{9,10},{10,1... | collective-permute-start | bytes 393224 | tf_op jit(solution)/shard_map/ppermute | solution.py:30
  30.8 2.6 %collective-permute-start.7 = (f32[8,32,128]{2,1,0:T(8,128)S(1)}, f32[8,32,128]{2,1,0:T(8,128)S(1)}, u32[]{:S(2)}, u32[]{:S(2)}) collective-permute-start(f32[8,32,128]{2,1,0:T(8,128)S(1)} %all-to-all-done.refs_7_), channel_id=1, source_target_pairs={{0,2},{1,3},{2,0},{3,1},{4,6},{5,7},{6,4},{7,5},{8,10},{9,11},{10,... | collective-permute-start | bytes 393224 | tf_op jit(solution)/shard_map/ppermute | solution.py:30
  33.4 1.1 %collective-permute-start.8 = (f32[8,32,128]{2,1,0:T(8,128)S(1)}, f32[8,32,128]{2,1,0:T(8,128)S(1)}, u32[]{:S(2)}, u32[]{:S(2)}) collective-permute-start(f32[8,32,128]{2,1,0:T(8,128)S(1)} %all-to-all-done.refs_7_), channel_id=1, source_target_pairs={{0,3},{1,0},{2,1},{3,2},{4,7},{5,4},{6,5},{7,6},{8,11},{9,8},{10,9... | collective-permute-start | bytes 393224 | tf_op jit(solution)/shard_map/ppermute | solution.py:30
  34.5 0.0 collective-permute-done.5.refs_6_.came
  34.5 0.0 copy-start.4
  34.5 0.0 copy-start.6
  34.5 0.1 collective-permute-start.10
  34.6 1.5 %collective-permute-start.9 = (f32[32,1024]{1,0:T(8,128)S(1)}, f32[32,1024]{1,0:T(8,128)S(1)}, u32[]{:S(2)}, u32[]{:S(2)}) collective-permute-start(f32[32,1024]{1,0:T(8,128)S(1)} %shard_map.75), channel_id=1, source_target_pairs={{0,32},{32,64},{64,96},{96,128},{128,160},{160,192},{192,224},{224... | collective-permute-start | bytes 393224 | tf_op jit(solution)/shard_map/ppermute | solution.py:30
  36.2 1.0 %collective-permute-done.7.refs_9_ = f32[8,32,128]{2,1,0:T(8,128)S(1)} collective-permute-done((f32[8,32,128]{2,1,0:T(8,128)S(1)}, f32[8,32,128]{2,1,0:T(8,128)S(1)}, u32[]{:S(2)}, u32[]{:S(2)}) %collective-permute-start.7) | collective-permute-done | bytes 131104 | tf_op jit(solution)/shard_map/ppermute | solution.py:30
  37.2 0.1 collective-permute-done.8.refs_10_
  37.2 1.8 %shard_map.74 = (f32[256,1024]{1,0:T(8,128)S(1)}, bf16[512,1024]{1,0:T(8,128)(2,1)S(1)}, bf16[512,1024]{1,0:T(8,128)(2,1)S(1)}, bf16[256,128]{1,0:T(8,128)(2,1)S(1)}, bf16[256,128]{1,0:T(8,128)(2,1)S(1)}) custom-call(f32[4,4]{1,0:T(4,128)S(1)} %copy-done.4, f32[64,1024]{1,0:T(8,128)S(1)} %copy-done.6, f32[64,1024]{1,0:T(8,128)S(1)} %collective-permute-done.refs_1_, ...), custom_call_target="tpu_custom_call" | custom-call | flops 805306368 | bytes 5636160 | tf_op jit(solution)/shard_map/pallas_call | solution.py:194
  39.1 0.7 collective-permute-done.9.top
  39.7 0.6 shard_map.77
  40.3 6.3 %collective-permute-start.11 = (f32[256,512]{1,0:T(8,128)S(1)}, f32[256,512]{1,0:T(8,128)S(1)}, u32[]{:S(2)}, u32[]{:S(2)}) collective-permute-start(f32[256,512]{1,0:T(8,128)S(1)} %get-tuple-element.34), channel_id=1, source_target_pairs={{0,4},{4,0},{1,5},{5,1},{2,6},{6,2},{3,7},{7,3},{8,12},{12,8},{9,1... | collective-permute-start | bytes 1572872 | tf_op jit(solution)/shard_map/ppermute | solution.py:30
  46.7 1.5 %collective-permute-done.11.received = f32[256,512]{1,0:T(8,128)S(1)} collective-permute-done((f32[256,512]{1,0:T(8,128)S(1)}, f32[256,512]{1,0:T(8,128)S(1)}, u32[]{:S(2)}, u32[]{:S(2)}) %collective-permute-start.11) | collective-permute-done | bytes 524320 | tf_op jit(solution)/shard_map/ppermute | solution.py:30
  48.2 0.1 shard_map.78
  48.3 1.3 %collective-permute-start.12 = (f32[256,128]{1,0:T(8,128)S(1)}, f32[256,128]{1,0:T(8,128)S(1)}, u32[]{:S(2)}, u32[]{:S(2)}) collective-permute-start(f32[256,128]{1,0:T(8,128)S(1)} %get-tuple-element.36), channel_id=1, source_target_pairs={{0,8},{8,16},{16,24},{24,0},{1,9},{9,17},{17,25},{25,1},{2,10},{10... | collective-permute-start | bytes 393224 | tf_op jit(solution)/shard_map/ppermute | solution.py:30
  49.6 2.5 %collective-permute-start.13 = (f32[256,128]{1,0:T(8,128)S(1)}, f32[256,128]{1,0:T(8,128)S(1)}, u32[]{:S(2)}, u32[]{:S(2)}) collective-permute-start(f32[256,128]{1,0:T(8,128)S(1)} %get-tuple-element.37), channel_id=1, source_target_pairs={{0,16},{8,24},{16,0},{24,8},{1,17},{9,25},{17,1},{25,9},{2,18},{10... | collective-permute-start | bytes 393224 | tf_op jit(solution)/shard_map/ppermute | solution.py:30
  52.1 1.2 %collective-permute-start.14 = (f32[256,128]{1,0:T(8,128)S(1)}, f32[256,128]{1,0:T(8,128)S(1)}, u32[]{:S(2)}, u32[]{:S(2)}) collective-permute-start(f32[256,128]{1,0:T(8,128)S(1)} %get-tuple-element.38), channel_id=1, source_target_pairs={{0,24},{8,0},{16,8},{24,16},{1,25},{9,1},{17,9},{25,17},{2,26},{10... | collective-permute-start | bytes 393224 | tf_op jit(solution)/shard_map/ppermute | solution.py:30
  53.2 0.6 copy-done.5
  53.9 0.7 shard_map.79.divisor
  54.6 3.5 %collective-permute-done.13.c = f32[256,128]{1,0:T(8,128)S(1)} collective-permute-done((f32[256,128]{1,0:T(8,128)S(1)}, f32[256,128]{1,0:T(8,128)S(1)}, u32[]{:S(2)}, u32[]{:S(2)}) %collective-permute-start.13) | collective-permute-done | bytes 131104 | tf_op jit(solution)/shard_map/ppermute | solution.py:30
  58.1 1.4 %collective-permute-start.15 = (f32[256,128]{1,0:T(8,128)S(1)}, f32[256,128]{1,0:T(8,128)S(1)}, u32[]{:S(2)}, u32[]{:S(2)}) collective-permute-start(f32[256,128]{1,0:T(8,128)S(1)} %shard_map.80.refs_0_), channel_id=1, source_target_pairs={{0,8},{8,16},{16,24},{24,0},{1,9},{9,17},{17,25},{25,1},{2,10},{10... | collective-permute-start | bytes 393224 | tf_op jit(solution)/shard_map/ppermute | solution.py:30
  59.5 2.1 %collective-permute-start.16 = (f32[256,128]{1,0:T(8,128)S(1)}, f32[256,128]{1,0:T(8,128)S(1)}, u32[]{:S(2)}, u32[]{:S(2)}) collective-permute-start(f32[256,128]{1,0:T(8,128)S(1)} %shard_map.80.refs_0_), channel_id=1, source_target_pairs={{0,16},{8,24},{16,0},{24,8},{1,17},{9,25},{17,1},{25,9},{2,18},{10... | collective-permute-start | bytes 393224 | tf_op jit(solution)/shard_map/ppermute | solution.py:30
  61.6 0.8 collective-permute-start.17
  62.4 2.3 %collective-permute-start.18 = (f32[256,128]{1,0:T(8,128)S(1)}, f32[256,128]{1,0:T(8,128)S(1)}, u32[]{:S(2)}, u32[]{:S(2)}) collective-permute-start(f32[256,128]{1,0:T(8,128)S(1)} %shard_map.80.refs_0_), channel_id=1, source_target_pairs={{0,4},{4,0},{1,5},{5,1},{2,6},{6,2},{3,7},{7,3},{8,12},{12,8},{9,1... | collective-permute-start | bytes 393224 | tf_op jit(solution)/shard_map/ppermute | solution.py:30
  64.7 2.0 %collective-permute-start.19 = (f32[256,128]{1,0:T(8,128)S(1)}, f32[256,128]{1,0:T(8,128)S(1)}, u32[]{:S(2)}, u32[]{:S(2)}) collective-permute-start(f32[256,128]{1,0:T(8,128)S(1)} %collective-permute-done.15.refs_1_), channel_id=1, source_target_pairs={{0,4},{4,0},{1,5},{5,1},{2,6},{6,2},{3,7},{7,3},{8,12},{12,8},{9,1... | collective-permute-start | bytes 393224 | tf_op jit(solution)/shard_map/ppermute | solution.py:30
  66.7 2.1 %collective-permute-start.20 = (f32[256,128]{1,0:T(8,128)S(1)}, f32[256,128]{1,0:T(8,128)S(1)}, u32[]{:S(2)}, u32[]{:S(2)}) collective-permute-start(f32[256,128]{1,0:T(8,128)S(1)} %collective-permute-done.16.refs_2_), channel_id=1, source_target_pairs={{0,4},{4,0},{1,5},{5,1},{2,6},{6,2},{3,7},{7,3},{8,12},{12,8},{9,1... | collective-permute-start | bytes 393224 | tf_op jit(solution)/shard_map/ppermute | solution.py:30
  68.9 0.1 collective-permute-start.21
  68.9 0.9 collective-permute-done.20.refs_6_
  69.8 0.4 collective-permute-done.21.refs_7_
  70.2 2.1 %shard_map.81 = (f32[8,32,128]{2,1,0:T(8,128)S(1)}, f32[8,32,128]{2,1,0:T(8,128)S(1)}, f32[8,32,128]{2,1,0:T(8,128)S(1)}, f32[8,32,128]{2,1,0:T(8,128)S(1)}) custom-call(f32[4,4]{1,0:T(4,128)S(1)} %copy-done.4, bf16[512,1024]{1,0:T(8,128)(2,1)S(1)} %get-tuple-element.26.z_high, bf16[512,1024]{1,0:T(8,128)(2,1)S(1)} %get-tuple-element.27.z_low, ...), custom_call_target="tpu_custom_call" | custom-call | flops 805306368 | bytes 3932224 | tf_op jit(solution)/shard_map/pallas_call | solution.py:194
  72.3 0.5 collective-permute-start.22
  72.8 2.0 %collective-permute-start.23 = (f32[8,32,128]{2,1,0:T(8,128)S(1)}, f32[8,32,128]{2,1,0:T(8,128)S(1)}, u32[]{:S(2)}, u32[]{:S(2)}) collective-permute-start(f32[8,32,128]{2,1,0:T(8,128)S(1)} %get-tuple-element.41), channel_id=1, source_target_pairs={{0,2},{1,3},{2,0},{3,1},{4,6},{5,7},{6,4},{7,5},{8,10},{9,11},{10,... | collective-permute-start | bytes 393224 | tf_op jit(solution)/shard_map/ppermute | solution.py:30
  74.8 0.6 collective-permute-start.24
  75.4 3.4 %collective-permute-done.22 = f32[8,32,128]{2,1,0:T(8,128)S(1)} collective-permute-done((f32[8,32,128]{2,1,0:T(8,128)S(1)}, f32[8,32,128]{2,1,0:T(8,128)S(1)}, u32[]{:S(2)}, u32[]{:S(2)}) %collective-permute-start.22) | collective-permute-done | bytes 131104 | tf_op jit(solution)/shard_map/ppermute | solution.py:30
  78.8 2.3 %collective-permute-done.23 = f32[8,32,128]{2,1,0:T(8,128)S(1)} collective-permute-done((f32[8,32,128]{2,1,0:T(8,128)S(1)}, f32[8,32,128]{2,1,0:T(8,128)S(1)}, u32[]{:S(2)}, u32[]{:S(2)}) %collective-permute-start.23) | collective-permute-done | bytes 131104 | tf_op jit(solution)/shard_map/ppermute | solution.py:30
  81.1 0.6 collective-permute-done.24
  81.7 11.6 %all_to_all.10.packed = f32[8,32,128]{2,1,0:T(8,128)S(1)} all-to-all(f32[8,32,128]{2,1,0:T(8,128)S(1)} %add_add_fusion), channel_id=1, replica_groups=mesh['z'=8,'x'=4,'core'=2,'y'=4] {'z'}, dimensions={0} | all-to-all | bytes 262144 | tf_op jit(solution)/shard_map/all_to_all | solution.py:268
  93.3 1.3 %shard_map.82 = f32[64,512]{1,0:T(8,128)} custom-call(f32[8,32,128]{2,1,0:T(8,128)S(1)} %all_to_all.10.packed, bf16[512,512]{1,0:T(8,128)(2,1)S(1)} %copy-done, bf16[512,512]{1,0:T(8,128)(2,1)S(1)} %copy-done.1), custom_call_target="tpu_custom_call" | custom-call | flops 100663296 | bytes 1310720 | tf_op jit(solution)/shard_map/pallas_call | solution.py:194
  (30 shorter events, 0.2 us)
Async XLA Ops:
  0.0 11.7 %collective-permute-start.3 = (f32[64,1024]{1,0:T(8,128)}, f32[64,1024]{1,0:T(8,128)S(1)}, u32[]{:S(2)}, u32[]{:S(2)}) collective-permute-start(f32[64,1024]{1,0:T(8,128)} %refs_0_.1), channel_id=1, source_target_pairs={{0,224},{32,0},{64,32},{96,64},{128,96},{160,128},{192,160},{224,1... | collective-permute-start | bytes 786440 | tf_op jit(solution)/shard_map/ppermute | solution.py:30
  6.4 8.6 %collective-permute-start = (f32[64,1024]{1,0:T(8,128)}, f32[64,1024]{1,0:T(8,128)S(1)}, u32[]{:S(2)}, u32[]{:S(2)}) collective-permute-start(f32[64,1024]{1,0:T(8,128)} %refs_0_.1), channel_id=1, source_target_pairs={{0,32},{32,64},{64,96},{96,128},{128,160},{160,192},{192,224},{224... | collective-permute-start | bytes 786440 | tf_op jit(solution)/shard_map/ppermute | solution.py:30
  11.7 9.7 %collective-permute-start.4 = (f32[64,1024]{1,0:T(8,128)S(1)}, f32[64,1024]{1,0:T(8,128)S(1)}, u32[]{:S(2)}, u32[]{:S(2)}) collective-permute-start(f32[64,1024]{1,0:T(8,128)S(1)} %collective-permute-done.3.refs_4_), channel_id=1, source_target_pairs={{0,224},{32,0},{64,32},{96,64},{128,96},{160,128},{192,160},{224,1... | collective-permute-start | bytes 786440 | tf_op jit(solution)/shard_map/ppermute | solution.py:30
  15.0 9.1 %collective-permute-start.1 = (f32[64,1024]{1,0:T(8,128)S(1)}, f32[64,1024]{1,0:T(8,128)S(1)}, u32[]{:S(2)}, u32[]{:S(2)}) collective-permute-start(f32[64,1024]{1,0:T(8,128)S(1)} %collective-permute-done.refs_1_), channel_id=1, source_target_pairs={{0,32},{32,64},{64,96},{96,128},{128,160},{160,192},{192,224},{224... | collective-permute-start | bytes 786440 | tf_op jit(solution)/shard_map/ppermute | solution.py:30
  17.4 12.0 %all-to-all-start = ((f32[8,32,128]{2,1,0:T(8,128)}), f32[8,32,128]{2,1,0:T(8,128)S(1)}, u32[]{:S(2)}, u32[]{:S(2)}) async-start(f32[8,32,128]{2,1,0:T(8,128)} %get-tuple-element.25), calls=%async_computation | async-start | bytes 262144 | tf_op jit(solution)/shard_map/all_to_all | solution.py:221
  21.4 13.1 %collective-permute-start.5 = (f32[64,1024]{1,0:T(8,128)S(1)}, f32[64,1024]{1,0:T(8,128)S(1)}, u32[]{:S(2)}, u32[]{:S(2)}) collective-permute-start(f32[64,1024]{1,0:T(8,128)S(1)} %collective-permute-done.4.refs_5_), channel_id=1, source_target_pairs={{0,224},{32,0},{64,32},{96,64},{128,96},{160,128},{192,160},{224,1... | collective-permute-start | bytes 786440 | tf_op jit(solution)/shard_map/ppermute | solution.py:30
  24.1 10.5 %collective-permute-start.2 = (f32[64,1024]{1,0:T(8,128)S(1)}, f32[64,1024]{1,0:T(8,128)S(1)}, u32[]{:S(2)}, u32[]{:S(2)}) collective-permute-start(f32[64,1024]{1,0:T(8,128)S(1)} %collective-permute-done.1.refs_2_), channel_id=1, source_target_pairs={{0,32},{32,64},{64,96},{96,128},{128,160},{160,192},{192,224},{224... | collective-permute-start | bytes 786440 | tf_op jit(solution)/shard_map/ppermute | solution.py:30
  29.5 6.7 %collective-permute-start.6 = (f32[8,32,128]{2,1,0:T(8,128)S(1)}, f32[8,32,128]{2,1,0:T(8,128)S(1)}, u32[]{:S(2)}, u32[]{:S(2)}) collective-permute-start(f32[8,32,128]{2,1,0:T(8,128)S(1)} %all-to-all-done.refs_7_), channel_id=1, source_target_pairs={{0,1},{1,2},{2,3},{3,0},{4,5},{5,6},{6,7},{7,4},{8,9},{9,10},{10,1... | collective-permute-start | bytes 393224 | tf_op jit(solution)/shard_map/ppermute | solution.py:30
  30.8 6.4 %collective-permute-start.7 = (f32[8,32,128]{2,1,0:T(8,128)S(1)}, f32[8,32,128]{2,1,0:T(8,128)S(1)}, u32[]{:S(2)}, u32[]{:S(2)}) collective-permute-start(f32[8,32,128]{2,1,0:T(8,128)S(1)} %all-to-all-done.refs_7_), channel_id=1, source_target_pairs={{0,2},{1,3},{2,0},{3,1},{4,6},{5,7},{6,4},{7,5},{8,10},{9,11},{10,... | collective-permute-start | bytes 393224 | tf_op jit(solution)/shard_map/ppermute | solution.py:30
  33.4 3.8 %collective-permute-start.8 = (f32[8,32,128]{2,1,0:T(8,128)S(1)}, f32[8,32,128]{2,1,0:T(8,128)S(1)}, u32[]{:S(2)}, u32[]{:S(2)}) collective-permute-start(f32[8,32,128]{2,1,0:T(8,128)S(1)} %all-to-all-done.refs_7_), channel_id=1, source_target_pairs={{0,3},{1,0},{2,1},{3,2},{4,7},{5,4},{6,5},{7,6},{8,11},{9,8},{10,9... | collective-permute-start | bytes 393224 | tf_op jit(solution)/shard_map/ppermute | solution.py:30
  34.5 2.7 %copy-start.4 = (f32[4,4]{1,0:T(4,128)S(1)}, f32[4,4]{1,0:T(4,128)}, u32[]{:S(2)}) copy-start(f32[4,4]{1,0:T(4,128)} %x_vectors.3) | copy-start | bytes 196
  34.5 2.7 %copy-start.6 = (f32[64,1024]{1,0:T(8,128)S(1)}, f32[64,1024]{1,0:T(8,128)}, u32[]{:S(2)}) copy-start(f32[64,1024]{1,0:T(8,128)} %refs_0_.1) | copy-start | bytes 786436
  34.5 4.6 %collective-permute-start.10 = (f32[32,1024]{1,0:T(8,128)S(1)}, f32[32,1024]{1,0:T(8,128)S(1)}, u32[]{:S(2)}, u32[]{:S(2)}) collective-permute-start(f32[32,1024]{1,0:T(8,128)S(1)} %shard_map.76), channel_id=1, source_target_pairs={{0,224},{32,0},{64,32},{96,64},{128,96},{160,128},{192,160},{224,1... | collective-permute-start | bytes 393224 | tf_op jit(solution)/shard_map/ppermute | solution.py:30
  34.6 5.1 %collective-permute-start.9 = (f32[32,1024]{1,0:T(8,128)S(1)}, f32[32,1024]{1,0:T(8,128)S(1)}, u32[]{:S(2)}, u32[]{:S(2)}) collective-permute-start(f32[32,1024]{1,0:T(8,128)S(1)} %shard_map.75), channel_id=1, source_target_pairs={{0,32},{32,64},{64,96},{96,128},{128,160},{160,192},{192,224},{224... | collective-permute-start | bytes 393224 | tf_op jit(solution)/shard_map/ppermute | solution.py:30
  40.3 7.8 %collective-permute-start.11 = (f32[256,512]{1,0:T(8,128)S(1)}, f32[256,512]{1,0:T(8,128)S(1)}, u32[]{:S(2)}, u32[]{:S(2)}) collective-permute-start(f32[256,512]{1,0:T(8,128)S(1)} %get-tuple-element.34), channel_id=1, source_target_pairs={{0,4},{4,0},{1,5},{5,1},{2,6},{6,2},{3,7},{7,3},{8,12},{12,8},{9,1... | collective-permute-start | bytes 1572872 | tf_op jit(solution)/shard_map/ppermute | solution.py:30
  48.2 5.0 %copy-start.2 = (f32[4096]{0:T(1024)S(1)}, f32[4096]{0:T(1024)}, u32[]{:S(2)}) copy-start(f32[4096]{0:T(1024)} %param.11) | copy-start | bytes 49156
  48.3 6.2 %collective-permute-start.12 = (f32[256,128]{1,0:T(8,128)S(1)}, f32[256,128]{1,0:T(8,128)S(1)}, u32[]{:S(2)}, u32[]{:S(2)}) collective-permute-start(f32[256,128]{1,0:T(8,128)S(1)} %get-tuple-element.36), channel_id=1, source_target_pairs={{0,8},{8,16},{16,24},{24,0},{1,9},{9,17},{17,25},{25,1},{2,10},{10... | collective-permute-start | bytes 393224 | tf_op jit(solution)/shard_map/ppermute | solution.py:30
  49.6 8.5 %collective-permute-start.13 = (f32[256,128]{1,0:T(8,128)S(1)}, f32[256,128]{1,0:T(8,128)S(1)}, u32[]{:S(2)}, u32[]{:S(2)}) collective-permute-start(f32[256,128]{1,0:T(8,128)S(1)} %get-tuple-element.37), channel_id=1, source_target_pairs={{0,16},{8,24},{16,0},{24,8},{1,17},{9,25},{17,1},{25,9},{2,18},{10... | collective-permute-start | bytes 393224 | tf_op jit(solution)/shard_map/ppermute | solution.py:30
  52.1 1.2 %copy-start.3 = (f32[512]{0:T(512)S(1)}, f32[512]{0:T(512)}, u32[]{:S(2)}) copy-start(f32[512]{0:T(512)} %param.13) | copy-start | bytes 6148
  52.1 6.0 %collective-permute-start.14 = (f32[256,128]{1,0:T(8,128)S(1)}, f32[256,128]{1,0:T(8,128)S(1)}, u32[]{:S(2)}, u32[]{:S(2)}) collective-permute-start(f32[256,128]{1,0:T(8,128)S(1)} %get-tuple-element.38), channel_id=1, source_target_pairs={{0,24},{8,0},{16,8},{24,16},{1,25},{9,1},{17,9},{25,17},{2,26},{10... | collective-permute-start | bytes 393224 | tf_op jit(solution)/shard_map/ppermute | solution.py:30
  53.2 0.7 copy-start.5
  58.1 6.6 %collective-permute-start.15 = (f32[256,128]{1,0:T(8,128)S(1)}, f32[256,128]{1,0:T(8,128)S(1)}, u32[]{:S(2)}, u32[]{:S(2)}) collective-permute-start(f32[256,128]{1,0:T(8,128)S(1)} %shard_map.80.refs_0_), channel_id=1, source_target_pairs={{0,8},{8,16},{16,24},{24,0},{1,9},{9,17},{17,25},{25,1},{2,10},{10... | collective-permute-start | bytes 393224 | tf_op jit(solution)/shard_map/ppermute | solution.py:30
  59.5 7.2 %collective-permute-start.16 = (f32[256,128]{1,0:T(8,128)S(1)}, f32[256,128]{1,0:T(8,128)S(1)}, u32[]{:S(2)}, u32[]{:S(2)}) collective-permute-start(f32[256,128]{1,0:T(8,128)S(1)} %shard_map.80.refs_0_), channel_id=1, source_target_pairs={{0,16},{8,24},{16,0},{24,8},{1,17},{9,25},{17,1},{25,9},{2,18},{10... | collective-permute-start | bytes 393224 | tf_op jit(solution)/shard_map/ppermute | solution.py:30
  61.6 7.3 %collective-permute-start.17 = (f32[256,128]{1,0:T(8,128)S(1)}, f32[256,128]{1,0:T(8,128)S(1)}, u32[]{:S(2)}, u32[]{:S(2)}) collective-permute-start(f32[256,128]{1,0:T(8,128)S(1)} %shard_map.80.refs_0_), channel_id=1, source_target_pairs={{0,24},{8,0},{16,8},{24,16},{1,25},{9,1},{17,9},{25,17},{2,26},{10... | collective-permute-start | bytes 393224 | tf_op jit(solution)/shard_map/ppermute | solution.py:30
  62.4 6.5 %collective-permute-start.18 = (f32[256,128]{1,0:T(8,128)S(1)}, f32[256,128]{1,0:T(8,128)S(1)}, u32[]{:S(2)}, u32[]{:S(2)}) collective-permute-start(f32[256,128]{1,0:T(8,128)S(1)} %shard_map.80.refs_0_), channel_id=1, source_target_pairs={{0,4},{4,0},{1,5},{5,1},{2,6},{6,2},{3,7},{7,3},{8,12},{12,8},{9,1... | collective-permute-start | bytes 393224 | tf_op jit(solution)/shard_map/ppermute | solution.py:30
  64.7 4.2 %collective-permute-start.19 = (f32[256,128]{1,0:T(8,128)S(1)}, f32[256,128]{1,0:T(8,128)S(1)}, u32[]{:S(2)}, u32[]{:S(2)}) collective-permute-start(f32[256,128]{1,0:T(8,128)S(1)} %collective-permute-done.15.refs_1_), channel_id=1, source_target_pairs={{0,4},{4,0},{1,5},{5,1},{2,6},{6,2},{3,7},{7,3},{8,12},{12,8},{9,1... | collective-permute-start | bytes 393224 | tf_op jit(solution)/shard_map/ppermute | solution.py:30
  66.7 3.1 %collective-permute-start.20 = (f32[256,128]{1,0:T(8,128)S(1)}, f32[256,128]{1,0:T(8,128)S(1)}, u32[]{:S(2)}, u32[]{:S(2)}) collective-permute-start(f32[256,128]{1,0:T(8,128)S(1)} %collective-permute-done.16.refs_2_), channel_id=1, source_target_pairs={{0,4},{4,0},{1,5},{5,1},{2,6},{6,2},{3,7},{7,3},{8,12},{12,8},{9,1... | collective-permute-start | bytes 393224 | tf_op jit(solution)/shard_map/ppermute | solution.py:30
  68.9 1.3 %collective-permute-start.21 = (f32[256,128]{1,0:T(8,128)S(1)}, f32[256,128]{1,0:T(8,128)S(1)}, u32[]{:S(2)}, u32[]{:S(2)}) collective-permute-start(f32[256,128]{1,0:T(8,128)S(1)} %collective-permute-done.17.refs_3_), channel_id=1, source_target_pairs={{0,4},{4,0},{1,5},{5,1},{2,6},{6,2},{3,7},{7,3},{8,12},{12,8},{9,1... | collective-permute-start | bytes 393224 | tf_op jit(solution)/shard_map/ppermute | solution.py:30
  70.2 23.0 %copy-start.1 = (bf16[512,512]{1,0:T(8,128)(2,1)S(1)}, bf16[512,512]{1,0:T(8,128)(2,1)}, u32[]{:S(2)}) copy-start(bf16[512,512]{1,0:T(8,128)(2,1)} %get-tuple-element.44.y_low) | copy-start | bytes 1572868
  72.3 20.9 %copy-start = (bf16[512,512]{1,0:T(8,128)(2,1)S(1)}, bf16[512,512]{1,0:T(8,128)(2,1)}, u32[]{:S(2)}) copy-start(bf16[512,512]{1,0:T(8,128)(2,1)} %get-tuple-element.43.y_high) | copy-start | bytes 1572868
  72.3 6.5 %collective-permute-start.22 = (f32[8,32,128]{2,1,0:T(8,128)S(1)}, f32[8,32,128]{2,1,0:T(8,128)S(1)}, u32[]{:S(2)}, u32[]{:S(2)}) collective-permute-start(f32[8,32,128]{2,1,0:T(8,128)S(1)} %get-tuple-element.40), channel_id=1, source_target_pairs={{0,1},{1,2},{2,3},{3,0},{4,5},{5,6},{6,7},{7,4},{8,9},{9,10},{10,1... | collective-permute-start | bytes 393224 | tf_op jit(solution)/shard_map/ppermute | solution.py:30
  72.8 8.2 %collective-permute-start.23 = (f32[8,32,128]{2,1,0:T(8,128)S(1)}, f32[8,32,128]{2,1,0:T(8,128)S(1)}, u32[]{:S(2)}, u32[]{:S(2)}) collective-permute-start(f32[8,32,128]{2,1,0:T(8,128)S(1)} %get-tuple-element.41), channel_id=1, source_target_pairs={{0,2},{1,3},{2,0},{3,1},{4,6},{5,7},{6,4},{7,5},{8,10},{9,11},{10,... | collective-permute-start | bytes 393224 | tf_op jit(solution)/shard_map/ppermute | solution.py:30
  74.8 6.9 %collective-permute-start.24 = (f32[8,32,128]{2,1,0:T(8,128)S(1)}, f32[8,32,128]{2,1,0:T(8,128)S(1)}, u32[]{:S(2)}, u32[]{:S(2)}) collective-permute-start(f32[8,32,128]{2,1,0:T(8,128)S(1)} %get-tuple-element.42), channel_id=1, source_target_pairs={{0,3},{1,0},{2,1},{3,2},{4,7},{5,4},{6,5},{7,6},{8,11},{9,8},{10,9... | collective-permute-start | bytes 393224 | tf_op jit(solution)/shard_map/ppermute | solution.py:30
where the time goes:
time: 95.7 us; the launch traced here: 94.5 us
  starting transfers between devices  47.9 us (50%)
  waiting for transfers between devices  25.1 us (26%)
  blocking collectives  11.6 us (12%)
  Pallas kernels  9.07 us (9%)
    ppermute x25, starting transfers between devices, shifted(): return lax.ppermute(value, axis, [(i, (i + step) % n) for i in range(n)])  43.9 us
    ppermute x25, waiting for transfers between devices, shifted(): return lax.ppermute(value, axis, [(i, (i + step) % n) for i in range(n)])  19.7 us
    all_to_all x1, blocking collectives, shards(): back = lax.all_to_all(mine, 'z', 0, 0, tiled=True)  11.6 us
    pallas_call x10, Pallas kernels, call(): pl.pallas_call(kernel, out_shape=out_shape, in_specs=[SMEM] * smem + [hel...  9.07 us
    all_to_all x1, waiting for transfers between devices, shards(): plane = lax.all_to_all(packed, 'z', 0, 0, tiled=True)  5.4 us
    all_to_all x1, starting transfers between devices, shards(): plane = lax.all_to_all(packed, 'z', 0, 0, tiled=True)  3.96 us
  transfers between devices with their start and end apart: 26, of which 12 were waited for; matrix products, arithmetic and copies ran while one was open for 0% of the time, Pallas kernels for 5%

commit v1 on v0

--- a/solution.py
+++ b/solution.py
@@ -101,6 +101,11 @@
         out[64 * i : 64 * i + 64] = (of_z + x_values[i]) + of_y
 
 
+def turned_kernel(high, low, high_out, low_out):
+    high_out[...] = high[...].T
+    low_out[...] = low[...].T
+
+
 def half_kernel(first, came, out):
     out[...] = came[first : first + 32]
 
@@ -131,17 +136,23 @@
         partial[:, lanes] = product((high, low), (z_high[:, lanes], z_low[:, lanes]), NN)
 
 
-def forward_far_kernel(partial, field_high, field_low, top, bottom, to_partner, kept, far_high, far_low):
-    core = lax.axis_index("core")
+def far_added(partial, field_high, field_low, far_high, far_low, half, out):
+    field = field_high[:, :64], field_low[:, :64]
+    for tile in range(2):
+        lanes = pl.ds(pl.multiple_of(half * 512 + tile * 256, 256), 256)
+        out[:, 256 * tile : 256 * tile + 256] = partial[:, lanes] + product(
+            field, (far_high[:, lanes], far_low[:, lanes]), NN
+        )
+
+
+def to_partner_kernel(partial, field_high, field_low, top, bottom, out, far_high, far_low):
     far_high[:32], far_low[:32] = two_parts(top[...])
     far_high[32:], far_low[32:] = two_parts(bottom[...])
-    field = field_high[:, :64], field_low[:, :64]
-    for out, half in ((to_partner, 1 - core), (kept, core)):
-        for tile in range(2):
-            lanes = pl.ds(pl.multiple_of(half * 512 + tile * 256, 256), 256)
-            out[:, 256 * tile : 256 * tile + 256] = partial[:, lanes] + product(
-                field, (far_high[:, lanes], far_low[:, lanes]), NN
-            )
+    far_added(partial, field_high, field_low, far_high, far_low, 1 - lax.axis_index("core"), out)
+
+
+def kept_kernel(partial, field_high, field_low, far_high, far_low, out):
+    far_added(partial, field_high, field_low, far_high, far_low, lax.axis_index("core"), out)
 
 
 def by_owner_kernel(kept, received, *outs):
@@ -154,38 +165,48 @@
     out[...] = ((a[...] + b[...]) + (c[...] + d[...])) / divisor[...]
 
 
-def backward_kernel(x_vectors, z_high, z_low, far_high, far_low, *refs):
-    blocks, outs, (s_high, s_low, first_high, first_low) = refs[:8], refs[8:12], refs[12:]
+def half_products(half, z_high, z_low, far_high, far_low, blocks, scratch):
+    s_high, s_low, first_high, first_low = scratch
+    of_half = pl.ds(pl.multiple_of(half * 512, 512), 512)
     for first, far, whole in ((first_high, far_high, z_high), (first_low, far_low, z_low)):
-        first[:64] = far[...]
-        first[64:] = whole[64:256]
-    core = lax.axis_index("core")
-    for number, block in enumerate(blocks):
-        half = core if number < 4 else 1 - core
-        lanes = pl.ds(pl.multiple_of(half * 512 + place("x", -number) * 128, 128), 128)
+        first[:64] = far[:, of_half]
+        first[64:] = whole[64:256, of_half]
+    for s, block in enumerate(blocks):
+        lanes = pl.ds(pl.multiple_of(place("x", -s) * 128, 128), 128)
         s_high[:, lanes], s_low[:, lanes] = two_parts(block[...])
     modes = s_high[...], s_low[...]
+    yield product((first_high[...], first_low[...]), modes, NT)
+    yield product((z_high[256:, of_half], z_low[256:, of_half]), modes, NT)
+
+
+def backward_own_kernel(z_high, z_low, far_high, far_low, *refs):
+    blocks, out, scratch = refs[:4], refs[4], refs[5:]
+    half = lax.axis_index("core")
+    for number, part in enumerate(half_products(half, z_high, z_low, far_high, far_low, blocks, scratch)):
+        out[256 * number : 256 * number + 256] = part
+
+
+def backward_kernel(x_vectors, own, z_high, z_low, far_high, far_low, *refs):
+    blocks, outs, scratch = refs[:4], refs[4:8], refs[8:]
+    half = 1 - lax.axis_index("core")
     weights = [[x_vectors[place("y", s), i] for i in range(4)] for s in range(4)]
-    for p in range(8):
-        at = 64 * (p % 4)
-        if p == 0:
-            part = product((first_high[...], first_low[...]), modes, NT)
-        elif p == 4:
-            part = product((z_high[256:], z_low[256:]), modes, NT)
-        packed = []
-        for pair in range(2):
-            lanes = slice(128 * pair, 128 * pair + 128)
-            packed += swapped_in(part[at : at + 32, lanes], part[at + 32 : at + 64, lanes])
-        block = place("z", OFFSETS[p])
-        for s, out in enumerate(outs):
-            out[block] = mixed(weights[s], packed)
+    for number, part in enumerate(half_products(half, z_high, z_low, far_high, far_low, blocks, scratch)):
+        whole = part + own[256 * number : 256 * number + 256]
+        for p in range(4):
+            packed = []
+            for pair in range(2):
+                lanes = slice(128 * pair, 128 * pair + 128)
+                packed += swapped_in(whole[64 * p : 64 * p + 32, lanes], whole[64 * p + 32 : 64 * p + 64, lanes])
+            block = place("z", OFFSETS[4 * number + p])
+            for s, out in enumerate(outs):
+                out[block] = mixed(weights[s], packed)
 
 
 def along_y_back_kernel(packed, y_high, y_low, out, field):
     for g in range(NZ_CHIPS // 2):
         lanes = slice(128 * g, 128 * g + 128)
         field[:32, lanes], field[32:, lanes] = swapped_in(packed[2 * g], packed[2 * g + 1])
-    out[...] = product(two_parts(field[...]), (y_high[...], y_low[...]), NT)
+    out[...] = product(two_parts(field[...]), (y_high[...], y_low[...]), NN)
 
 
 def call(kernel, out_shape, operands, smem=0, scratch=(), flops=0, vmem=16 << 20, held=VMEM):
@@ -219,6 +240,7 @@
     right1 = shifted(z_vectors, "z", 1)
     left1 = shifted(z_vectors, "z", -1)
     plane = lax.all_to_all(packed, "z", 0, 0, tiled=True)
+    y_high, y_low = call(turned_kernel, (bf16(512, 512),) * 2, (y_high, y_low))
     divisor = call(
         divisor_kernel,
         f32(256, 128),
@@ -241,13 +263,17 @@
         scratch=[pltpu.VMEM((512, 256), jnp.float32)],
         flops=2 * 512 * 256 * 1024 * 3,
     )
-    to_partner, kept, far_high, far_low = call(
-        forward_far_kernel,
-        (f32(256, 512), f32(256, 512), bf16(64, 1024), bf16(64, 1024)),
-        (partial, field_high, field_low, top, bottom),
-        flops=2 * 64 * 256 * 1024 * 3,
+    field = field_high, field_low
+    to_partner, far_high, far_low = call(
+        to_partner_kernel,
+        (f32(256, 512), bf16(64, 1024), bf16(64, 1024)),
+        (partial, *field, top, bottom),
+        flops=64 * 256 * 1024 * 3,
     )
     received = shifted(to_partner, "core", 1)
+    kept = call(
+        kept_kernel, f32(256, 512), (partial, *field, far_high, far_low), flops=64 * 256 * 1024 * 3
+    )
     mine, *others = call(by_owner_kernel, (f32(256, 128),) * 4, (kept, received))
     sums = [shifted(part, "x", s) for s, part in enumerate(others, 1)]
     scaled = call(scaled_kernel, f32(256, 128), (mine, *sums, divisor))
@@ -255,13 +281,21 @@
     modes = [scaled] + [shifted(scaled, "x", s) for s in (1, 2, 3)]
     across = [shifted(block, "core", 1) for block in modes]
     z_parts = z_high, z_low, far_high, far_low
+    scratch = [pltpu.VMEM((256, 512), jnp.bfloat16)] * 4
+    own = call(
+        backward_own_kernel,
+        f32(512, 256),
+        (*z_parts, *modes),
+        scratch=scratch,
+        flops=512 * 256 * 1024 * 3,
+    )
     mine, *others = call(
         backward_kernel,
         (f32(8, 32, 128),) * 4,
-        (x_vectors, *z_parts, *modes, *across),
+        (x_vectors, own, *z_parts, *across),
         smem=1,
-        scratch=[pltpu.VMEM((256, 1024), jnp.bfloat16)] * 4,
-        flops=2 * 512 * 256 * 1024 * 3,
+        scratch=scratch,
+        flops=512 * 256 * 1024 * 3,
     )
     for s, part in enumerate(others, 1):
         mine = mine + shifted(part, "y", s)

time: 95.7 us -> 95.6 us (level)
  blocking collectives: 11.6 us -> 0 us
  waiting for transfers between devices: 25.1 us -> 31.6 us
  starting transfers between devices: 47.9 us -> 51.7 us
    all_to_all x1 -> x0, blocking collectives: 11.6 us -> none  [shards(): back = lax.all_to_all(mine, 'z', 0, 0, tiled=True)]
    all_to_all x0 -> x1, waiting for transfers between devices: none -> 7.61 us  [shards(): back = lax.all_to_all(mine, 'z', 0, 0, tiled=True)]
    all_to_all x0 -> x1, starting transfers between devices: none -> 3.82 us  [shards(): back = lax.all_to_all(mine, 'z', 0, 0, tiled=True)]
    ppermute x25, waiting for transfers between devices: 19.7 us -> 18.6 us  [shifted(): return lax.ppermute(value, axis, [(i, (i + step) % n) for i in range(n)])]
    pallas_call x10 -> x13, Pallas kernels: 9.07 us -> 9.36 us  [call(): pl.pallas_call(kernel, out_shape=out_shape, in_specs=[SMEM] * smem + [hel...]
  transfers between devices with their start and end apart: 26 -> 27, of which waited for: 12 -> 13; matrix products, arithmetic and copies ran while one was open for 0% -> 0% of each run, Pallas kernels for 5% -> 7%
where the time goes in v1:
time: 95.6 us; the launch traced here: 94.3 us
  starting transfers between devices  51.7 us (54%)
  waiting for transfers between devices  31.6 us (33%)
  Pallas kernels  9.36 us (10%)
    ppermute x25, starting transfers between devices, shifted(): return lax.ppermute(value, axis, [(i, (i + step) % n) for i in range(n)])  44 us
    ppermute x25, waiting for transfers between devices, shifted(): return lax.ppermute(value, axis, [(i, (i + step) % n) for i in range(n)])  18.6 us
    pallas_call x13, Pallas kernels, call(): pl.pallas_call(kernel, out_shape=out_shape, in_specs=[SMEM] * smem + [hel...  9.36 us
    all_to_all x1, waiting for transfers between devices, shards(): back = lax.all_to_all(mine, 'z', 0, 0, tiled=True)  7.61 us
    all_to_all x1, waiting for transfers between devices, shards(): plane = lax.all_to_all(packed, 'z', 0, 0, tiled=True)  5.4 us
    all_to_all x1, starting transfers between devices, shards(): plane = lax.all_to_all(packed, 'z', 0, 0, tiled=True)  3.96 us
    all_to_all x1, starting transfers between devices, shards(): back = lax.all_to_all(mine, 'z', 0, 0, tiled=True)  3.82 us
  transfers between devices with their start and end apart: 27, of which 13 were waited for; matrix products, arithmetic and copies ran while one was open for 0% of the time, Pallas kernels for 7%

profile of v1, /device:TPU:1, one launch (start us, length us, event | category | flops | bytes accessed | tf_op | source)
XLA Modules:
  0.0 94.3 jit_solution(13628201988724382470)
XLA Ops:
  0.0 6.4 %collective-permute-start.3 = (f32[64,1024]{1,0:T(8,128)}, f32[64,1024]{1,0:T(8,128)S(1)}, u32[]{:S(2)}, u32[]{:S(2)}) collective-permute-start(f32[64,1024]{1,0:T(8,128)} %refs_0_.1), channel_id=1, source_target_pairs={{0,224},{32,0},{64,32},{96,64},{128,96},{160,128},{192,160},{224,1... | collective-permute-start | bytes 786440 | tf_op jit(solution)/shard_map/ppermute | solution.py:30
  6.4 5.3 %collective-permute-done.3.refs_4_ = f32[64,1024]{1,0:T(8,128)S(1)} collective-permute-done((f32[64,1024]{1,0:T(8,128)}, f32[64,1024]{1,0:T(8,128)S(1)}, u32[]{:S(2)}, u32[]{:S(2)}) %collective-permute-start.3) | collective-permute-done | bytes 262176 | tf_op jit(solution)/shard_map/ppermute | solution.py:30
  11.7 3.3 %collective-permute-start.4 = (f32[64,1024]{1,0:T(8,128)S(1)}, f32[64,1024]{1,0:T(8,128)S(1)}, u32[]{:S(2)}, u32[]{:S(2)}) collective-permute-start(f32[64,1024]{1,0:T(8,128)S(1)} %collective-permute-done.3.refs_4_), channel_id=1, source_target_pairs={{0,224},{32,0},{64,32},{96,64},{128,96},{160,128},{192,160},{224,1... | collective-permute-start | bytes 786440 | tf_op jit(solution)/shard_map/ppermute | solution.py:30
  15.0 2.4 %shard_map.73 = (f32[8,32,128]{2,1,0:T(8,128)}, bf16[512,512]{1,0:T(8,128)(2,1)}, bf16[512,512]{1,0:T(8,128)(2,1)}) custom-call(f32[64,512]{1,0:T(8,128)} %source.1, f32[512,512]{1,0:T(8,128)} %y_vectors.1), custom_call_target="tpu_custom_call" | custom-call | flops 100663296 | bytes 2359296 | tf_op jit(solution)/shard_map/pallas_call | solution.py:215
  17.4 4.0 %all-to-all-start = ((f32[8,32,128]{2,1,0:T(8,128)}), f32[8,32,128]{2,1,0:T(8,128)S(1)}, u32[]{:S(2)}, u32[]{:S(2)}) async-start(f32[8,32,128]{2,1,0:T(8,128)} %get-tuple-element.26), calls=%async_computation | async-start | bytes 262144 | tf_op jit(solution)/shard_map/all_to_all | solution.py:242
  21.4 2.7 %collective-permute-start.5 = (f32[64,1024]{1,0:T(8,128)S(1)}, f32[64,1024]{1,0:T(8,128)S(1)}, u32[]{:S(2)}, u32[]{:S(2)}) collective-permute-start(f32[64,1024]{1,0:T(8,128)S(1)} %collective-permute-done.4.refs_5_), channel_id=1, source_target_pairs={{0,224},{32,0},{64,32},{96,64},{128,96},{160,128},{192,160},{224,1... | collective-permute-start | bytes 786440 | tf_op jit(solution)/shard_map/ppermute | solution.py:30
  24.1 5.4 %all-to-all-done.refs_7_ = f32[8,32,128]{2,1,0:T(8,128)S(1)} async-done(((f32[8,32,128]{2,1,0:T(8,128)}), f32[8,32,128]{2,1,0:T(8,128)S(1)}, u32[]{:S(2)}, u32[]{:S(2)}) %all-to-all-start) | async-done | bytes 131104 | tf_op jit(solution)/shard_map/all_to_all | solution.py:242
  29.5 1.3 %collective-permute-start.6 = (f32[8,32,128]{2,1,0:T(8,128)S(1)}, f32[8,32,128]{2,1,0:T(8,128)S(1)}, u32[]{:S(2)}, u32[]{:S(2)}) collective-permute-start(f32[8,32,128]{2,1,0:T(8,128)S(1)} %all-to-all-done.refs_7_), channel_id=1, source_target_pairs={{0,1},{1,2},{2,3},{3,0},{4,5},{5,6},{6,7},{7,4},{8,9},{9,10},{10,1... | collective-permute-start | bytes 393224 | tf_op jit(solution)/shard_map/ppermute | solution.py:30
  30.8 2.6 %collective-permute-start.7 = (f32[8,32,128]{2,1,0:T(8,128)S(1)}, f32[8,32,128]{2,1,0:T(8,128)S(1)}, u32[]{:S(2)}, u32[]{:S(2)}) collective-permute-start(f32[8,32,128]{2,1,0:T(8,128)S(1)} %all-to-all-done.refs_7_), channel_id=1, source_target_pairs={{0,2},{1,3},{2,0},{3,1},{4,6},{5,7},{6,4},{7,5},{8,10},{9,11},{10,... | collective-permute-start | bytes 393224 | tf_op jit(solution)/shard_map/ppermute | solution.py:30
  33.4 1.1 %collective-permute-start.8 = (f32[8,32,128]{2,1,0:T(8,128)S(1)}, f32[8,32,128]{2,1,0:T(8,128)S(1)}, u32[]{:S(2)}, u32[]{:S(2)}) collective-permute-start(f32[8,32,128]{2,1,0:T(8,128)S(1)} %all-to-all-done.refs_7_), channel_id=1, source_target_pairs={{0,3},{1,0},{2,1},{3,2},{4,7},{5,4},{6,5},{7,6},{8,11},{9,8},{10,9... | collective-permute-start | bytes 393224 | tf_op jit(solution)/shard_map/ppermute | solution.py:30
  34.5 0.1 collective-permute-start.10
  34.6 1.5 %collective-permute-start.9 = (f32[32,1024]{1,0:T(8,128)S(1)}, f32[32,1024]{1,0:T(8,128)S(1)}, u32[]{:S(2)}, u32[]{:S(2)}) collective-permute-start(f32[32,1024]{1,0:T(8,128)S(1)} %shard_map.75), channel_id=1, source_target_pairs={{0,32},{32,64},{64,96},{96,128},{128,160},{160,192},{192,224},{224... | collective-permute-start | bytes 393224 | tf_op jit(solution)/shard_map/ppermute | solution.py:30
  36.2 1.0 %collective-permute-done.7.refs_9_ = f32[8,32,128]{2,1,0:T(8,128)S(1)} collective-permute-done((f32[8,32,128]{2,1,0:T(8,128)S(1)}, f32[8,32,128]{2,1,0:T(8,128)S(1)}, u32[]{:S(2)}, u32[]{:S(2)}) %collective-permute-start.7) | collective-permute-done | bytes 131104 | tf_op jit(solution)/shard_map/ppermute | solution.py:30
  37.2 0.1 collective-permute-done.8.refs_10_
  37.2 1.8 %shard_map.74 = (f32[256,1024]{1,0:T(8,128)S(1)}, bf16[512,1024]{1,0:T(8,128)(2,1)S(1)}, bf16[512,1024]{1,0:T(8,128)(2,1)S(1)}, bf16[256,128]{1,0:T(8,128)(2,1)S(1)}, bf16[256,128]{1,0:T(8,128)(2,1)S(1)}) custom-call(f32[4,4]{1,0:T(4,128)S(1)} %copy-done.4, f32[64,1024]{1,0:T(8,128)S(1)} %copy-done.6, f32[64,1024]{1,0:T(8,128)S(1)} %collective-permute-done.refs_1_, ...), custom_call_target="tpu_custom_call" | custom-call | flops 805306368 | bytes 5636160 | tf_op jit(solution)/shard_map/pallas_call | solution.py:215
  39.1 0.7 collective-permute-done.9.top
  39.7 0.4 shard_map.77
  40.1 6.3 %collective-permute-start.11 = (f32[256,512]{1,0:T(8,128)S(1)}, f32[256,512]{1,0:T(8,128)S(1)}, u32[]{:S(2)}, u32[]{:S(2)}) collective-permute-start(f32[256,512]{1,0:T(8,128)S(1)} %get-tuple-element.34), channel_id=1, source_target_pairs={{0,4},{4,0},{1,5},{5,1},{2,6},{6,2},{3,7},{7,3},{8,12},{12,8},{9,1... | collective-permute-start | bytes 1572872 | tf_op jit(solution)/shard_map/ppermute | solution.py:30
  46.4 0.3 shard_map.78.kept
  46.8 1.2 %collective-permute-done.11.received = f32[256,512]{1,0:T(8,128)S(1)} collective-permute-done((f32[256,512]{1,0:T(8,128)S(1)}, f32[256,512]{1,0:T(8,128)S(1)}, u32[]{:S(2)}, u32[]{:S(2)}) %collective-permute-start.11) | collective-permute-done | bytes 524320 | tf_op jit(solution)/shard_map/ppermute | solution.py:30
  48.0 0.1 shard_map.79
  48.1 1.3 %collective-permute-start.12 = (f32[256,128]{1,0:T(8,128)S(1)}, f32[256,128]{1,0:T(8,128)S(1)}, u32[]{:S(2)}, u32[]{:S(2)}) collective-permute-start(f32[256,128]{1,0:T(8,128)S(1)} %get-tuple-element.36), channel_id=1, source_target_pairs={{0,8},{8,16},{16,24},{24,0},{1,9},{9,17},{17,25},{25,1},{2,10},{10... | collective-permute-start | bytes 393224 | tf_op jit(solution)/shard_map/ppermute | solution.py:30
  49.4 2.4 %collective-permute-start.13 = (f32[256,128]{1,0:T(8,128)S(1)}, f32[256,128]{1,0:T(8,128)S(1)}, u32[]{:S(2)}, u32[]{:S(2)}) collective-permute-start(f32[256,128]{1,0:T(8,128)S(1)} %get-tuple-element.37), channel_id=1, source_target_pairs={{0,16},{8,24},{16,0},{24,8},{1,17},{9,25},{17,1},{25,9},{2,18},{10... | collective-permute-start | bytes 393224 | tf_op jit(solution)/shard_map/ppermute | solution.py:30
  51.9 1.2 %collective-permute-start.14 = (f32[256,128]{1,0:T(8,128)S(1)}, f32[256,128]{1,0:T(8,128)S(1)}, u32[]{:S(2)}, u32[]{:S(2)}) collective-permute-start(f32[256,128]{1,0:T(8,128)S(1)} %get-tuple-element.38), channel_id=1, source_target_pairs={{0,24},{8,0},{16,8},{24,16},{1,25},{9,1},{17,9},{25,17},{2,26},{10... | collective-permute-start | bytes 393224 | tf_op jit(solution)/shard_map/ppermute | solution.py:30
  53.0 0.6 copy-done.5
  53.7 0.7 shard_map.80.divisor
  54.4 3.5 %collective-permute-done.13.c = f32[256,128]{1,0:T(8,128)S(1)} collective-permute-done((f32[256,128]{1,0:T(8,128)S(1)}, f32[256,128]{1,0:T(8,128)S(1)}, u32[]{:S(2)}, u32[]{:S(2)}) %collective-permute-start.13) | collective-permute-done | bytes 131104 | tf_op jit(solution)/shard_map/ppermute | solution.py:30
  57.9 1.4 %collective-permute-start.15 = (f32[256,128]{1,0:T(8,128)S(1)}, f32[256,128]{1,0:T(8,128)S(1)}, u32[]{:S(2)}, u32[]{:S(2)}) collective-permute-start(f32[256,128]{1,0:T(8,128)S(1)} %shard_map.81.refs_0_), channel_id=1, source_target_pairs={{0,8},{8,16},{16,24},{24,0},{1,9},{9,17},{17,25},{25,1},{2,10},{10... | collective-permute-start | bytes 393224 | tf_op jit(solution)/shard_map/ppermute | solution.py:30
  59.3 2.1 %collective-permute-start.16 = (f32[256,128]{1,0:T(8,128)S(1)}, f32[256,128]{1,0:T(8,128)S(1)}, u32[]{:S(2)}, u32[]{:S(2)}) collective-permute-start(f32[256,128]{1,0:T(8,128)S(1)} %shard_map.81.refs_0_), channel_id=1, source_target_pairs={{0,16},{8,24},{16,0},{24,8},{1,17},{9,25},{17,1},{25,9},{2,18},{10... | collective-permute-start | bytes 393224 | tf_op jit(solution)/shard_map/ppermute | solution.py:30
  61.4 0.8 collective-permute-start.17
  62.2 2.3 %collective-permute-start.18 = (f32[256,128]{1,0:T(8,128)S(1)}, f32[256,128]{1,0:T(8,128)S(1)}, u32[]{:S(2)}, u32[]{:S(2)}) collective-permute-start(f32[256,128]{1,0:T(8,128)S(1)} %shard_map.81.refs_0_), channel_id=1, source_target_pairs={{0,4},{4,0},{1,5},{5,1},{2,6},{6,2},{3,7},{7,3},{8,12},{12,8},{9,1... | collective-permute-start | bytes 393224 | tf_op jit(solution)/shard_map/ppermute | solution.py:30
  64.5 2.0 %collective-permute-start.19 = (f32[256,128]{1,0:T(8,128)S(1)}, f32[256,128]{1,0:T(8,128)S(1)}, u32[]{:S(2)}, u32[]{:S(2)}) collective-permute-start(f32[256,128]{1,0:T(8,128)S(1)} %collective-permute-done.15.refs_1_), channel_id=1, source_target_pairs={{0,4},{4,0},{1,5},{5,1},{2,6},{6,2},{3,7},{7,3},{8,12},{12,8},{9,1... | collective-permute-start | bytes 393224 | tf_op jit(solution)/shard_map/ppermute | solution.py:30
  66.5 2.1 %collective-permute-start.20 = (f32[256,128]{1,0:T(8,128)S(1)}, f32[256,128]{1,0:T(8,128)S(1)}, u32[]{:S(2)}, u32[]{:S(2)}) collective-permute-start(f32[256,128]{1,0:T(8,128)S(1)} %collective-permute-done.16.refs_2_), channel_id=1, source_target_pairs={{0,4},{4,0},{1,5},{5,1},{2,6},{6,2},{3,7},{7,3},{8,12},{12,8},{9,1... | collective-permute-start | bytes 393224 | tf_op jit(solution)/shard_map/ppermute | solution.py:30
  68.7 0.7 shard_map.82.own
  69.4 0.2 collective-permute-done.20.refs_2_
  69.6 0.4 collective-permute-done.21.refs_3_
  70.0 1.4 %shard_map.83 = (f32[8,32,128]{2,1,0:T(8,128)S(1)}, f32[8,32,128]{2,1,0:T(8,128)S(1)}, f32[8,32,128]{2,1,0:T(8,128)S(1)}, f32[8,32,128]{2,1,0:T(8,128)S(1)}) custom-call(f32[4,4]{1,0:T(4,128)S(1)} %copy-done.4, f32[512,256]{1,0:T(8,128)S(1)} %shard_map.82.own, bf16[512,1024]{1,0:T(8,128)(2,1)S(1)} %get-tuple-element.27.z_high, ...), custom_call_target="tpu_custom_call" | custom-call | flops 402653184 | bytes 3932224 | tf_op jit(solution)/shard_map/pallas_call | solution.py:215
  71.5 0.5 collective-permute-start.22
  71.9 2.0 %collective-permute-start.23 = (f32[8,32,128]{2,1,0:T(8,128)S(1)}, f32[8,32,128]{2,1,0:T(8,128)S(1)}, u32[]{:S(2)}, u32[]{:S(2)}) collective-permute-start(f32[8,32,128]{2,1,0:T(8,128)S(1)} %get-tuple-element.41), channel_id=1, source_target_pairs={{0,2},{1,3},{2,0},{3,1},{4,6},{5,7},{6,4},{7,5},{8,10},{9,11},{10,... | collective-permute-start | bytes 393224 | tf_op jit(solution)/shard_map/ppermute | solution.py:30
  73.9 0.6 collective-permute-start.24
  74.5 3.4 %collective-permute-done.22 = f32[8,32,128]{2,1,0:T(8,128)S(1)} collective-permute-done((f32[8,32,128]{2,1,0:T(8,128)S(1)}, f32[8,32,128]{2,1,0:T(8,128)S(1)}, u32[]{:S(2)}, u32[]{:S(2)}) %collective-permute-start.22) | collective-permute-done | bytes 131104 | tf_op jit(solution)/shard_map/ppermute | solution.py:30
  77.9 2.3 %collective-permute-done.23 = f32[8,32,128]{2,1,0:T(8,128)S(1)} collective-permute-done((f32[8,32,128]{2,1,0:T(8,128)S(1)}, f32[8,32,128]{2,1,0:T(8,128)S(1)}, u32[]{:S(2)}, u32[]{:S(2)}) %collective-permute-start.23) | collective-permute-done | bytes 131104 | tf_op jit(solution)/shard_map/ppermute | solution.py:30
  80.2 0.6 collective-permute-done.24
  80.8 0.7 add_add_fusion
  81.5 3.8 %all-to-all-start.1 = ((f32[8,32,128]{2,1,0:T(8,128)}), f32[8,32,128]{2,1,0:T(8,128)S(1)}, u32[]{:S(2)}, u32[]{:S(2)}) async-start(f32[8,32,128]{2,1,0:T(8,128)} %add_add_fusion), calls=%async_computation.1 | async-start | bytes 262144 | tf_op jit(solution)/shard_map/all_to_all | solution.py:302
  85.3 0.3 shard_map.84
  85.6 7.6 %all-to-all-done.1.packed = f32[8,32,128]{2,1,0:T(8,128)S(1)} async-done(((f32[8,32,128]{2,1,0:T(8,128)}), f32[8,32,128]{2,1,0:T(8,128)S(1)}, u32[]{:S(2)}, u32[]{:S(2)}) %all-to-all-start.1) | async-done | bytes 131104 | tf_op jit(solution)/shard_map/all_to_all | solution.py:302
  93.2 1.1 %shard_map.85 = f32[64,512]{1,0:T(8,128)} custom-call(f32[8,32,128]{2,1,0:T(8,128)S(1)} %all-to-all-done.1.packed, bf16[512,512]{1,0:T(8,128)(2,1)S(1)} %get-tuple-element.45.y_high, bf16[512,512]{1,0:T(8,128)(2,1)S(1)} %get-tuple-element.46.y_low), custom_call_target="tpu_custom_call" | custom-call | flops 100663296 | bytes 1310720 | tf_op jit(solution)/shard_map/pallas_call | solution.py:215
  (34 shorter events, 0.2 us)
Async XLA Ops:
  0.0 11.7 %collective-permute-start.3 = (f32[64,1024]{1,0:T(8,128)}, f32[64,1024]{1,0:T(8,128)S(1)}, u32[]{:S(2)}, u32[]{:S(2)}) collective-permute-start(f32[64,1024]{1,0:T(8,128)} %refs_0_.1), channel_id=1, source_target_pairs={{0,224},{32,0},{64,32},{96,64},{128,96},{160,128},{192,160},{224,1... | collective-permute-start | bytes 786440 | tf_op jit(solution)/shard_map/ppermute | solution.py:30
  6.4 8.6 %collective-permute-start = (f32[64,1024]{1,0:T(8,128)}, f32[64,1024]{1,0:T(8,128)S(1)}, u32[]{:S(2)}, u32[]{:S(2)}) collective-permute-start(f32[64,1024]{1,0:T(8,128)} %refs_0_.1), channel_id=1, source_target_pairs={{0,32},{32,64},{64,96},{96,128},{128,160},{160,192},{192,224},{224... | collective-permute-start | bytes 786440 | tf_op jit(solution)/shard_map/ppermute | solution.py:30
  11.7 9.7 %collective-permute-start.4 = (f32[64,1024]{1,0:T(8,128)S(1)}, f32[64,1024]{1,0:T(8,128)S(1)}, u32[]{:S(2)}, u32[]{:S(2)}) collective-permute-start(f32[64,1024]{1,0:T(8,128)S(1)} %collective-permute-done.3.refs_4_), channel_id=1, source_target_pairs={{0,224},{32,0},{64,32},{96,64},{128,96},{160,128},{192,160},{224,1... | collective-permute-start | bytes 786440 | tf_op jit(solution)/shard_map/ppermute | solution.py:30
  15.0 9.1 %collective-permute-start.1 = (f32[64,1024]{1,0:T(8,128)S(1)}, f32[64,1024]{1,0:T(8,128)S(1)}, u32[]{:S(2)}, u32[]{:S(2)}) collective-permute-start(f32[64,1024]{1,0:T(8,128)S(1)} %collective-permute-done.refs_1_), channel_id=1, source_target_pairs={{0,32},{32,64},{64,96},{96,128},{128,160},{160,192},{192,224},{224... | collective-permute-start | bytes 786440 | tf_op jit(solution)/shard_map/ppermute | solution.py:30
  17.4 12.0 %all-to-all-start = ((f32[8,32,128]{2,1,0:T(8,128)}), f32[8,32,128]{2,1,0:T(8,128)S(1)}, u32[]{:S(2)}, u32[]{:S(2)}) async-start(f32[8,32,128]{2,1,0:T(8,128)} %get-tuple-element.26), calls=%async_computation | async-start | bytes 262144 | tf_op jit(solution)/shard_map/all_to_all | solution.py:242
  21.4 13.1 %collective-permute-start.5 = (f32[64,1024]{1,0:T(8,128)S(1)}, f32[64,1024]{1,0:T(8,128)S(1)}, u32[]{:S(2)}, u32[]{:S(2)}) collective-permute-start(f32[64,1024]{1,0:T(8,128)S(1)} %collective-permute-done.4.refs_5_), channel_id=1, source_target_pairs={{0,224},{32,0},{64,32},{96,64},{128,96},{160,128},{192,160},{224,1... | collective-permute-start | bytes 786440 | tf_op jit(solution)/shard_map/ppermute | solution.py:30
  24.1 10.5 %collective-permute-start.2 = (f32[64,1024]{1,0:T(8,128)S(1)}, f32[64,1024]{1,0:T(8,128)S(1)}, u32[]{:S(2)}, u32[]{:S(2)}) collective-permute-start(f32[64,1024]{1,0:T(8,128)S(1)} %collective-permute-done.1.refs_2_), channel_id=1, source_target_pairs={{0,32},{32,64},{64,96},{96,128},{128,160},{160,192},{192,224},{224... | collective-permute-start | bytes 786440 | tf_op jit(solution)/shard_map/ppermute | solution.py:30
  29.5 6.7 %collective-permute-start.6 = (f32[8,32,128]{2,1,0:T(8,128)S(1)}, f32[8,32,128]{2,1,0:T(8,128)S(1)}, u32[]{:S(2)}, u32[]{:S(2)}) collective-permute-start(f32[8,32,128]{2,1,0:T(8,128)S(1)} %all-to-all-done.refs_7_), channel_id=1, source_target_pairs={{0,1},{1,2},{2,3},{3,0},{4,5},{5,6},{6,7},{7,4},{8,9},{9,10},{10,1... | collective-permute-start | bytes 393224 | tf_op jit(solution)/shard_map/ppermute | solution.py:30
  30.8 6.4 %collective-permute-start.7 = (f32[8,32,128]{2,1,0:T(8,128)S(1)}, f32[8,32,128]{2,1,0:T(8,128)S(1)}, u32[]{:S(2)}, u32[]{:S(2)}) collective-permute-start(f32[8,32,128]{2,1,0:T(8,128)S(1)} %all-to-all-done.refs_7_), channel_id=1, source_target_pairs={{0,2},{1,3},{2,0},{3,1},{4,6},{5,7},{6,4},{7,5},{8,10},{9,11},{10,... | collective-permute-start | bytes 393224 | tf_op jit(solution)/shard_map/ppermute | solution.py:30
  33.4 3.8 %collective-permute-start.8 = (f32[8,32,128]{2,1,0:T(8,128)S(1)}, f32[8,32,128]{2,1,0:T(8,128)S(1)}, u32[]{:S(2)}, u32[]{:S(2)}) collective-permute-start(f32[8,32,128]{2,1,0:T(8,128)S(1)} %all-to-all-done.refs_7_), channel_id=1, source_target_pairs={{0,3},{1,0},{2,1},{3,2},{4,7},{5,4},{6,5},{7,6},{8,11},{9,8},{10,9... | collective-permute-start | bytes 393224 | tf_op jit(solution)/shard_map/ppermute | solution.py:30
  34.5 2.7 %copy-start.4 = (f32[4,4]{1,0:T(4,128)S(1)}, f32[4,4]{1,0:T(4,128)}, u32[]{:S(2)}) copy-start(f32[4,4]{1,0:T(4,128)} %x_vectors.3) | copy-start | bytes 196
  34.5 2.7 %copy-start.6 = (f32[64,1024]{1,0:T(8,128)S(1)}, f32[64,1024]{1,0:T(8,128)}, u32[]{:S(2)}) copy-start(f32[64,1024]{1,0:T(8,128)} %refs_0_.1) | copy-start | bytes 786436
  34.5 4.6 %collective-permute-start.10 = (f32[32,1024]{1,0:T(8,128)S(1)}, f32[32,1024]{1,0:T(8,128)S(1)}, u32[]{:S(2)}, u32[]{:S(2)}) collective-permute-start(f32[32,1024]{1,0:T(8,128)S(1)} %shard_map.76), channel_id=1, source_target_pairs={{0,224},{32,0},{64,32},{96,64},{128,96},{160,128},{192,160},{224,1... | collective-permute-start | bytes 393224 | tf_op jit(solution)/shard_map/ppermute | solution.py:30
  34.6 5.1 %collective-permute-start.9 = (f32[32,1024]{1,0:T(8,128)S(1)}, f32[32,1024]{1,0:T(8,128)S(1)}, u32[]{:S(2)}, u32[]{:S(2)}) collective-permute-start(f32[32,1024]{1,0:T(8,128)S(1)} %shard_map.75), channel_id=1, source_target_pairs={{0,32},{32,64},{64,96},{96,128},{128,160},{160,192},{192,224},{224... | collective-permute-start | bytes 393224 | tf_op jit(solution)/shard_map/ppermute | solution.py:30
  40.1 7.8 %collective-permute-start.11 = (f32[256,512]{1,0:T(8,128)S(1)}, f32[256,512]{1,0:T(8,128)S(1)}, u32[]{:S(2)}, u32[]{:S(2)}) collective-permute-start(f32[256,512]{1,0:T(8,128)S(1)} %get-tuple-element.34), channel_id=1, source_target_pairs={{0,4},{4,0},{1,5},{5,1},{2,6},{6,2},{3,7},{7,3},{8,12},{12,8},{9,1... | collective-permute-start | bytes 1572872 | tf_op jit(solution)/shard_map/ppermute | solution.py:30
  48.0 5.0 %copy-start.2 = (f32[4096]{0:T(1024)S(1)}, f32[4096]{0:T(1024)}, u32[]{:S(2)}) copy-start(f32[4096]{0:T(1024)} %param.11) | copy-start | bytes 49156
  48.1 6.2 %collective-permute-start.12 = (f32[256,128]{1,0:T(8,128)S(1)}, f32[256,128]{1,0:T(8,128)S(1)}, u32[]{:S(2)}, u32[]{:S(2)}) collective-permute-start(f32[256,128]{1,0:T(8,128)S(1)} %get-tuple-element.36), channel_id=1, source_target_pairs={{0,8},{8,16},{16,24},{24,0},{1,9},{9,17},{17,25},{25,1},{2,10},{10... | collective-permute-start | bytes 393224 | tf_op jit(solution)/shard_map/ppermute | solution.py:30
  49.4 8.5 %collective-permute-start.13 = (f32[256,128]{1,0:T(8,128)S(1)}, f32[256,128]{1,0:T(8,128)S(1)}, u32[]{:S(2)}, u32[]{:S(2)}) collective-permute-start(f32[256,128]{1,0:T(8,128)S(1)} %get-tuple-element.37), channel_id=1, source_target_pairs={{0,16},{8,24},{16,0},{24,8},{1,17},{9,25},{17,1},{25,9},{2,18},{10... | collective-permute-start | bytes 393224 | tf_op jit(solution)/shard_map/ppermute | solution.py:30
  51.9 1.2 %copy-start.3 = (f32[512]{0:T(512)S(1)}, f32[512]{0:T(512)}, u32[]{:S(2)}) copy-start(f32[512]{0:T(512)} %param.13) | copy-start | bytes 6148
  51.9 6.0 %collective-permute-start.14 = (f32[256,128]{1,0:T(8,128)S(1)}, f32[256,128]{1,0:T(8,128)S(1)}, u32[]{:S(2)}, u32[]{:S(2)}) collective-permute-start(f32[256,128]{1,0:T(8,128)S(1)} %get-tuple-element.38), channel_id=1, source_target_pairs={{0,24},{8,0},{16,8},{24,16},{1,25},{9,1},{17,9},{25,17},{2,26},{10... | collective-permute-start | bytes 393224 | tf_op jit(solution)/shard_map/ppermute | solution.py:30
  53.0 0.7 copy-start.5
  57.9 6.6 %collective-permute-start.15 = (f32[256,128]{1,0:T(8,128)S(1)}, f32[256,128]{1,0:T(8,128)S(1)}, u32[]{:S(2)}, u32[]{:S(2)}) collective-permute-start(f32[256,128]{1,0:T(8,128)S(1)} %shard_map.81.refs_0_), channel_id=1, source_target_pairs={{0,8},{8,16},{16,24},{24,0},{1,9},{9,17},{17,25},{25,1},{2,10},{10... | collective-permute-start | bytes 393224 | tf_op jit(solution)/shard_map/ppermute | solution.py:30
  59.3 7.2 %collective-permute-start.16 = (f32[256,128]{1,0:T(8,128)S(1)}, f32[256,128]{1,0:T(8,128)S(1)}, u32[]{:S(2)}, u32[]{:S(2)}) collective-permute-start(f32[256,128]{1,0:T(8,128)S(1)} %shard_map.81.refs_0_), channel_id=1, source_target_pairs={{0,16},{8,24},{16,0},{24,8},{1,17},{9,25},{17,1},{25,9},{2,18},{10... | collective-permute-start | bytes 393224 | tf_op jit(solution)/shard_map/ppermute | solution.py:30
  61.4 7.3 %collective-permute-start.17 = (f32[256,128]{1,0:T(8,128)S(1)}, f32[256,128]{1,0:T(8,128)S(1)}, u32[]{:S(2)}, u32[]{:S(2)}) collective-permute-start(f32[256,128]{1,0:T(8,128)S(1)} %shard_map.81.refs_0_), channel_id=1, source_target_pairs={{0,24},{8,0},{16,8},{24,16},{1,25},{9,1},{17,9},{25,17},{2,26},{10... | collective-permute-start | bytes 393224 | tf_op jit(solution)/shard_map/ppermute | solution.py:30
  62.2 7.2 %collective-permute-start.18 = (f32[256,128]{1,0:T(8,128)S(1)}, f32[256,128]{1,0:T(8,128)S(1)}, u32[]{:S(2)}, u32[]{:S(2)}) collective-permute-start(f32[256,128]{1,0:T(8,128)S(1)} %shard_map.81.refs_0_), channel_id=1, source_target_pairs={{0,4},{4,0},{1,5},{5,1},{2,6},{6,2},{3,7},{7,3},{8,12},{12,8},{9,1... | collective-permute-start | bytes 393224 | tf_op jit(solution)/shard_map/ppermute | solution.py:30
  64.5 4.9 %collective-permute-start.19 = (f32[256,128]{1,0:T(8,128)S(1)}, f32[256,128]{1,0:T(8,128)S(1)}, u32[]{:S(2)}, u32[]{:S(2)}) collective-permute-start(f32[256,128]{1,0:T(8,128)S(1)} %collective-permute-done.15.refs_1_), channel_id=1, source_target_pairs={{0,4},{4,0},{1,5},{5,1},{2,6},{6,2},{3,7},{7,3},{8,12},{12,8},{9,1... | collective-permute-start | bytes 393224 | tf_op jit(solution)/shard_map/ppermute | solution.py:30
  66.5 3.1 %collective-permute-start.20 = (f32[256,128]{1,0:T(8,128)S(1)}, f32[256,128]{1,0:T(8,128)S(1)}, u32[]{:S(2)}, u32[]{:S(2)}) collective-permute-start(f32[256,128]{1,0:T(8,128)S(1)} %collective-permute-done.16.refs_2_), channel_id=1, source_target_pairs={{0,4},{4,0},{1,5},{5,1},{2,6},{6,2},{3,7},{7,3},{8,12},{12,8},{9,1... | collective-permute-start | bytes 393224 | tf_op jit(solution)/shard_map/ppermute | solution.py:30
  68.7 1.3 %collective-permute-start.21 = (f32[256,128]{1,0:T(8,128)S(1)}, f32[256,128]{1,0:T(8,128)S(1)}, u32[]{:S(2)}, u32[]{:S(2)}) collective-permute-start(f32[256,128]{1,0:T(8,128)S(1)} %collective-permute-done.17.refs_3_), channel_id=1, source_target_pairs={{0,4},{4,0},{1,5},{5,1},{2,6},{6,2},{3,7},{7,3},{8,12},{12,8},{9,1... | collective-permute-start | bytes 393224 | tf_op jit(solution)/shard_map/ppermute | solution.py:30
  70.0 15.3 %copy-start.1 = (bf16[512,512]{1,0:T(8,128)(2,1)S(1)}, bf16[512,512]{1,0:T(8,128)(2,1)}, u32[]{:S(2)}) copy-start(bf16[512,512]{1,0:T(8,128)(2,1)} %get-tuple-element.44.low) | copy-start | bytes 1572868
  71.5 13.8 %copy-start = (bf16[512,512]{1,0:T(8,128)(2,1)S(1)}, bf16[512,512]{1,0:T(8,128)(2,1)}, u32[]{:S(2)}) copy-start(bf16[512,512]{1,0:T(8,128)(2,1)} %get-tuple-element.43.high) | copy-start | bytes 1572868
  71.5 6.4 %collective-permute-start.22 = (f32[8,32,128]{2,1,0:T(8,128)S(1)}, f32[8,32,128]{2,1,0:T(8,128)S(1)}, u32[]{:S(2)}, u32[]{:S(2)}) collective-permute-start(f32[8,32,128]{2,1,0:T(8,128)S(1)} %get-tuple-element.40), channel_id=1, source_target_pairs={{0,1},{1,2},{2,3},{3,0},{4,5},{5,6},{6,7},{7,4},{8,9},{9,10},{10,1... | collective-permute-start | bytes 393224 | tf_op jit(solution)/shard_map/ppermute | solution.py:30
  71.9 8.2 %collective-permute-start.23 = (f32[8,32,128]{2,1,0:T(8,128)S(1)}, f32[8,32,128]{2,1,0:T(8,128)S(1)}, u32[]{:S(2)}, u32[]{:S(2)}) collective-permute-start(f32[8,32,128]{2,1,0:T(8,128)S(1)} %get-tuple-element.41), channel_id=1, source_target_pairs={{0,2},{1,3},{2,0},{3,1},{4,6},{5,7},{6,4},{7,5},{8,10},{9,11},{10,... | collective-permute-start | bytes 393224 | tf_op jit(solution)/shard_map/ppermute | solution.py:30
  73.9 6.8 %collective-permute-start.24 = (f32[8,32,128]{2,1,0:T(8,128)S(1)}, f32[8,32,128]{2,1,0:T(8,128)S(1)}, u32[]{:S(2)}, u32[]{:S(2)}) collective-permute-start(f32[8,32,128]{2,1,0:T(8,128)S(1)} %get-tuple-element.42), channel_id=1, source_target_pairs={{0,3},{1,0},{2,1},{3,2},{4,7},{5,4},{6,5},{7,6},{8,11},{9,8},{10,9... | collective-permute-start | bytes 393224 | tf_op jit(solution)/shard_map/ppermute | solution.py:30
  81.5 11.8 %all-to-all-start.1 = ((f32[8,32,128]{2,1,0:T(8,128)}), f32[8,32,128]{2,1,0:T(8,128)S(1)}, u32[]{:S(2)}, u32[]{:S(2)}) async-start(f32[8,32,128]{2,1,0:T(8,128)} %add_add_fusion), calls=%async_computation.1 | async-start | bytes 262144 | tf_op jit(solution)/shard_map/all_to_all | solution.py:302

commit v2 on v1

--- a/solution.py
+++ b/solution.py
@@ -202,6 +202,10 @@
                 out[block] = mixed(weights[s], packed)
 
 
+def summed_kernel(a, b, c, d, out):
+    out[...] = (a[...] + b[...]) + (c[...] + d[...])
+
+
 def along_y_back_kernel(packed, y_high, y_low, out, field):
     for g in range(NZ_CHIPS // 2):
         lanes = slice(128 * g, 128 * g + 128)
@@ -297,8 +301,8 @@
         scratch=scratch,
         flops=512 * 256 * 1024 * 3,
     )
-    for s, part in enumerate(others, 1):
-        mine = mine + shifted(part, "y", s)
+    others = [shifted(part, "y", s) for s, part in enumerate(others, 1)]
+    mine = call(summed_kernel, f32(8, 32, 128), (mine, *others))
     back = lax.all_to_all(mine, "z", 0, 0, tiled=True)
     return call(
         along_y_back_kernel,

time: 95.6 us -> 95.6 us (level)
    pallas_call x13 -> x14, Pallas kernels: 9.36 us -> 10 us  [call(): pl.pallas_call(kernel, out_shape=out_shape, in_specs=[SMEM] * smem + [hel...]
where the time goes in v2:
time: 95.6 us; the launch traced here: 94.3 us
  starting transfers between devices  51.7 us (54%)
  waiting for transfers between devices  31.6 us (33%)
  Pallas kernels  10 us (10%)
    ppermute x25, starting transfers between devices, shifted(): return lax.ppermute(value, axis, [(i, (i + step) % n) for i in range(n)])  44 us
    ppermute x25, waiting for transfers between devices, shifted(): return lax.ppermute(value, axis, [(i, (i + step) % n) for i in range(n)])  18.6 us
    pallas_call x14, Pallas kernels, call(): pl.pallas_call(kernel, out_shape=out_shape, in_specs=[SMEM] * smem + [hel...  10 us
    all_to_all x1, waiting for transfers between devices, shards(): back = lax.all_to_all(mine, 'z', 0, 0, tiled=True)  7.61 us
    all_to_all x1, waiting for transfers between devices, shards(): plane = lax.all_to_all(packed, 'z', 0, 0, tiled=True)  5.4 us
    all_to_all x1, starting transfers between devices, shards(): plane = lax.all_to_all(packed, 'z', 0, 0, tiled=True)  3.96 us
    all_to_all x1, starting transfers between devices, shards(): back = lax.all_to_all(mine, 'z', 0, 0, tiled=True)  3.82 us
  transfers between devices with their start and end apart: 27, of which 13 were waited for; matrix products, arithmetic and copies ran while one was open for 0% of the time, Pallas kernels for 7%

profile of v2, /device:TPU:1, one launch (start us, length us, event | category | flops | bytes accessed | tf_op | source)
XLA Modules:
  0.0 94.3 jit_solution(900901550378610352)
XLA Ops:
  0.0 6.4 %collective-permute-start.3 = (f32[64,1024]{1,0:T(8,128)}, f32[64,1024]{1,0:T(8,128)S(1)}, u32[]{:S(2)}, u32[]{:S(2)}) collective-permute-start(f32[64,1024]{1,0:T(8,128)} %refs_0_.1), channel_id=1, source_target_pairs={{0,224},{32,0},{64,32},{96,64},{128,96},{160,128},{192,160},{224,1... | collective-permute-start | bytes 786440 | tf_op jit(solution)/shard_map/ppermute | solution.py:30
  6.4 5.3 %collective-permute-done.3.refs_4_ = f32[64,1024]{1,0:T(8,128)S(1)} collective-permute-done((f32[64,1024]{1,0:T(8,128)}, f32[64,1024]{1,0:T(8,128)S(1)}, u32[]{:S(2)}, u32[]{:S(2)}) %collective-permute-start.3) | collective-permute-done | bytes 262176 | tf_op jit(solution)/shard_map/ppermute | solution.py:30
  11.7 3.3 %collective-permute-start.4 = (f32[64,1024]{1,0:T(8,128)S(1)}, f32[64,1024]{1,0:T(8,128)S(1)}, u32[]{:S(2)}, u32[]{:S(2)}) collective-permute-start(f32[64,1024]{1,0:T(8,128)S(1)} %collective-permute-done.3.refs_4_), channel_id=1, source_target_pairs={{0,224},{32,0},{64,32},{96,64},{128,96},{160,128},{192,160},{224,1... | collective-permute-start | bytes 786440 | tf_op jit(solution)/shard_map/ppermute | solution.py:30
  15.0 2.4 %shard_map.73 = (f32[8,32,128]{2,1,0:T(8,128)}, bf16[512,512]{1,0:T(8,128)(2,1)}, bf16[512,512]{1,0:T(8,128)(2,1)}) custom-call(f32[64,512]{1,0:T(8,128)} %source.1, f32[512,512]{1,0:T(8,128)} %y_vectors.1), custom_call_target="tpu_custom_call" | custom-call | flops 100663296 | bytes 2359296 | tf_op jit(solution)/shard_map/pallas_call | solution.py:219
  17.4 4.0 %all-to-all-start = ((f32[8,32,128]{2,1,0:T(8,128)}), f32[8,32,128]{2,1,0:T(8,128)S(1)}, u32[]{:S(2)}, u32[]{:S(2)}) async-start(f32[8,32,128]{2,1,0:T(8,128)} %get-tuple-element.26), calls=%async_computation | async-start | bytes 262144 | tf_op jit(solution)/shard_map/all_to_all | solution.py:246
  21.4 2.7 %collective-permute-start.5 = (f32[64,1024]{1,0:T(8,128)S(1)}, f32[64,1024]{1,0:T(8,128)S(1)}, u32[]{:S(2)}, u32[]{:S(2)}) collective-permute-start(f32[64,1024]{1,0:T(8,128)S(1)} %collective-permute-done.4.refs_5_), channel_id=1, source_target_pairs={{0,224},{32,0},{64,32},{96,64},{128,96},{160,128},{192,160},{224,1... | collective-permute-start | bytes 786440 | tf_op jit(solution)/shard_map/ppermute | solution.py:30
  24.1 5.4 %all-to-all-done.refs_7_ = f32[8,32,128]{2,1,0:T(8,128)S(1)} async-done(((f32[8,32,128]{2,1,0:T(8,128)}), f32[8,32,128]{2,1,0:T(8,128)S(1)}, u32[]{:S(2)}, u32[]{:S(2)}) %all-to-all-start) | async-done | bytes 131104 | tf_op jit(solution)/shard_map/all_to_all | solution.py:246
  29.5 1.3 %collective-permute-start.6 = (f32[8,32,128]{2,1,0:T(8,128)S(1)}, f32[8,32,128]{2,1,0:T(8,128)S(1)}, u32[]{:S(2)}, u32[]{:S(2)}) collective-permute-start(f32[8,32,128]{2,1,0:T(8,128)S(1)} %all-to-all-done.refs_7_), channel_id=1, source_target_pairs={{0,1},{1,2},{2,3},{3,0},{4,5},{5,6},{6,7},{7,4},{8,9},{9,10},{10,1... | collective-permute-start | bytes 393224 | tf_op jit(solution)/shard_map/ppermute | solution.py:30
  30.8 2.6 %collective-permute-start.7 = (f32[8,32,128]{2,1,0:T(8,128)S(1)}, f32[8,32,128]{2,1,0:T(8,128)S(1)}, u32[]{:S(2)}, u32[]{:S(2)}) collective-permute-start(f32[8,32,128]{2,1,0:T(8,128)S(1)} %all-to-all-done.refs_7_), channel_id=1, source_target_pairs={{0,2},{1,3},{2,0},{3,1},{4,6},{5,7},{6,4},{7,5},{8,10},{9,11},{10,... | collective-permute-start | bytes 393224 | tf_op jit(solution)/shard_map/ppermute | solution.py:30
  33.4 1.1 %collective-permute-start.8 = (f32[8,32,128]{2,1,0:T(8,128)S(1)}, f32[8,32,128]{2,1,0:T(8,128)S(1)}, u32[]{:S(2)}, u32[]{:S(2)}) collective-permute-start(f32[8,32,128]{2,1,0:T(8,128)S(1)} %all-to-all-done.refs_7_), channel_id=1, source_target_pairs={{0,3},{1,0},{2,1},{3,2},{4,7},{5,4},{6,5},{7,6},{8,11},{9,8},{10,9... | collective-permute-start | bytes 393224 | tf_op jit(solution)/shard_map/ppermute | solution.py:30
  34.5 0.1 collective-permute-start.10
  34.6 1.5 %collective-permute-start.9 = (f32[32,1024]{1,0:T(8,128)S(1)}, f32[32,1024]{1,0:T(8,128)S(1)}, u32[]{:S(2)}, u32[]{:S(2)}) collective-permute-start(f32[32,1024]{1,0:T(8,128)S(1)} %shard_map.75), channel_id=1, source_target_pairs={{0,32},{32,64},{64,96},{96,128},{128,160},{160,192},{192,224},{224... | collective-permute-start | bytes 393224 | tf_op jit(solution)/shard_map/ppermute | solution.py:30
  36.2 1.0 %collective-permute-done.7.refs_9_ = f32[8,32,128]{2,1,0:T(8,128)S(1)} collective-permute-done((f32[8,32,128]{2,1,0:T(8,128)S(1)}, f32[8,32,128]{2,1,0:T(8,128)S(1)}, u32[]{:S(2)}, u32[]{:S(2)}) %collective-permute-start.7) | collective-permute-done | bytes 131104 | tf_op jit(solution)/shard_map/ppermute | solution.py:30
  37.2 0.1 collective-permute-done.8.refs_10_
  37.2 1.8 %shard_map.74 = (f32[256,1024]{1,0:T(8,128)S(1)}, bf16[512,1024]{1,0:T(8,128)(2,1)S(1)}, bf16[512,1024]{1,0:T(8,128)(2,1)S(1)}, bf16[256,128]{1,0:T(8,128)(2,1)S(1)}, bf16[256,128]{1,0:T(8,128)(2,1)S(1)}) custom-call(f32[4,4]{1,0:T(4,128)S(1)} %copy-done.4, f32[64,1024]{1,0:T(8,128)S(1)} %copy-done.6, f32[64,1024]{1,0:T(8,128)S(1)} %collective-permute-done.refs_1_, ...), custom_call_target="tpu_custom_call" | custom-call | flops 805306368 | bytes 5636160 | tf_op jit(solution)/shard_map/pallas_call | solution.py:219
  39.1 0.7 collective-permute-done.9.top
  39.7 0.4 shard_map.77
  40.1 6.3 %collective-permute-start.11 = (f32[256,512]{1,0:T(8,128)S(1)}, f32[256,512]{1,0:T(8,128)S(1)}, u32[]{:S(2)}, u32[]{:S(2)}) collective-permute-start(f32[256,512]{1,0:T(8,128)S(1)} %get-tuple-element.34), channel_id=1, source_target_pairs={{0,4},{4,0},{1,5},{5,1},{2,6},{6,2},{3,7},{7,3},{8,12},{12,8},{9,1... | collective-permute-start | bytes 1572872 | tf_op jit(solution)/shard_map/ppermute | solution.py:30
  46.4 0.3 shard_map.78.kept
  46.8 1.2 %collective-permute-done.11.received = f32[256,512]{1,0:T(8,128)S(1)} collective-permute-done((f32[256,512]{1,0:T(8,128)S(1)}, f32[256,512]{1,0:T(8,128)S(1)}, u32[]{:S(2)}, u32[]{:S(2)}) %collective-permute-start.11) | collective-permute-done | bytes 524320 | tf_op jit(solution)/shard_map/ppermute | solution.py:30
  48.0 0.1 shard_map.79
  48.1 1.3 %collective-permute-start.12 = (f32[256,128]{1,0:T(8,128)S(1)}, f32[256,128]{1,0:T(8,128)S(1)}, u32[]{:S(2)}, u32[]{:S(2)}) collective-permute-start(f32[256,128]{1,0:T(8,128)S(1)} %get-tuple-element.36), channel_id=1, source_target_pairs={{0,8},{8,16},{16,24},{24,0},{1,9},{9,17},{17,25},{25,1},{2,10},{10... | collective-permute-start | bytes 393224 | tf_op jit(solution)/shard_map/ppermute | solution.py:30
  49.4 2.4 %collective-permute-start.13 = (f32[256,128]{1,0:T(8,128)S(1)}, f32[256,128]{1,0:T(8,128)S(1)}, u32[]{:S(2)}, u32[]{:S(2)}) collective-permute-start(f32[256,128]{1,0:T(8,128)S(1)} %get-tuple-element.37), channel_id=1, source_target_pairs={{0,16},{8,24},{16,0},{24,8},{1,17},{9,25},{17,1},{25,9},{2,18},{10... | collective-permute-start | bytes 393224 | tf_op jit(solution)/shard_map/ppermute | solution.py:30
  51.9 1.2 %collective-permute-start.14 = (f32[256,128]{1,0:T(8,128)S(1)}, f32[256,128]{1,0:T(8,128)S(1)}, u32[]{:S(2)}, u32[]{:S(2)}) collective-permute-start(f32[256,128]{1,0:T(8,128)S(1)} %get-tuple-element.38), channel_id=1, source_target_pairs={{0,24},{8,0},{16,8},{24,16},{1,25},{9,1},{17,9},{25,17},{2,26},{10... | collective-permute-start | bytes 393224 | tf_op jit(solution)/shard_map/ppermute | solution.py:30
  53.0 0.6 copy-done.5
  53.7 0.7 shard_map.80.divisor
  54.4 3.5 %collective-permute-done.13.c = f32[256,128]{1,0:T(8,128)S(1)} collective-permute-done((f32[256,128]{1,0:T(8,128)S(1)}, f32[256,128]{1,0:T(8,128)S(1)}, u32[]{:S(2)}, u32[]{:S(2)}) %collective-permute-start.13) | collective-permute-done | bytes 131104 | tf_op jit(solution)/shard_map/ppermute | solution.py:30
  57.9 1.4 %collective-permute-start.15 = (f32[256,128]{1,0:T(8,128)S(1)}, f32[256,128]{1,0:T(8,128)S(1)}, u32[]{:S(2)}, u32[]{:S(2)}) collective-permute-start(f32[256,128]{1,0:T(8,128)S(1)} %shard_map.81.refs_0_), channel_id=1, source_target_pairs={{0,8},{8,16},{16,24},{24,0},{1,9},{9,17},{17,25},{25,1},{2,10},{10... | collective-permute-start | bytes 393224 | tf_op jit(solution)/shard_map/ppermute | solution.py:30
  59.3 2.1 %collective-permute-start.16 = (f32[256,128]{1,0:T(8,128)S(1)}, f32[256,128]{1,0:T(8,128)S(1)}, u32[]{:S(2)}, u32[]{:S(2)}) collective-permute-start(f32[256,128]{1,0:T(8,128)S(1)} %shard_map.81.refs_0_), channel_id=1, source_target_pairs={{0,16},{8,24},{16,0},{24,8},{1,17},{9,25},{17,1},{25,9},{2,18},{10... | collective-permute-start | bytes 393224 | tf_op jit(solution)/shard_map/ppermute | solution.py:30
  61.4 0.8 collective-permute-start.17
  62.2 2.3 %collective-permute-start.18 = (f32[256,128]{1,0:T(8,128)S(1)}, f32[256,128]{1,0:T(8,128)S(1)}, u32[]{:S(2)}, u32[]{:S(2)}) collective-permute-start(f32[256,128]{1,0:T(8,128)S(1)} %shard_map.81.refs_0_), channel_id=1, source_target_pairs={{0,4},{4,0},{1,5},{5,1},{2,6},{6,2},{3,7},{7,3},{8,12},{12,8},{9,1... | collective-permute-start | bytes 393224 | tf_op jit(solution)/shard_map/ppermute | solution.py:30
  64.5 2.0 %collective-permute-start.19 = (f32[256,128]{1,0:T(8,128)S(1)}, f32[256,128]{1,0:T(8,128)S(1)}, u32[]{:S(2)}, u32[]{:S(2)}) collective-permute-start(f32[256,128]{1,0:T(8,128)S(1)} %collective-permute-done.15.refs_1_), channel_id=1, source_target_pairs={{0,4},{4,0},{1,5},{5,1},{2,6},{6,2},{3,7},{7,3},{8,12},{12,8},{9,1... | collective-permute-start | bytes 393224 | tf_op jit(solution)/shard_map/ppermute | solution.py:30
  66.5 2.1 %collective-permute-start.20 = (f32[256,128]{1,0:T(8,128)S(1)}, f32[256,128]{1,0:T(8,128)S(1)}, u32[]{:S(2)}, u32[]{:S(2)}) collective-permute-start(f32[256,128]{1,0:T(8,128)S(1)} %collective-permute-done.16.refs_2_), channel_id=1, source_target_pairs={{0,4},{4,0},{1,5},{5,1},{2,6},{6,2},{3,7},{7,3},{8,12},{12,8},{9,1... | collective-permute-start | bytes 393224 | tf_op jit(solution)/shard_map/ppermute | solution.py:30
  68.7 0.7 shard_map.82.own
  69.4 0.2 collective-permute-done.20.refs_2_
  69.6 0.4 collective-permute-done.21.refs_3_
  70.0 1.4 %shard_map.83 = (f32[8,32,128]{2,1,0:T(8,128)S(1)}, f32[8,32,128]{2,1,0:T(8,128)S(1)}, f32[8,32,128]{2,1,0:T(8,128)S(1)}, f32[8,32,128]{2,1,0:T(8,128)S(1)}) custom-call(f32[4,4]{1,0:T(4,128)S(1)} %copy-done.4, f32[512,256]{1,0:T(8,128)S(1)} %shard_map.82.own, bf16[512,1024]{1,0:T(8,128)(2,1)S(1)} %get-tuple-element.27.z_high, ...), custom_call_target="tpu_custom_call" | custom-call | flops 402653184 | bytes 3932224 | tf_op jit(solution)/shard_map/pallas_call | solution.py:219
  71.5 0.5 collective-permute-start.22
  71.9 2.0 %collective-permute-start.23 = (f32[8,32,128]{2,1,0:T(8,128)S(1)}, f32[8,32,128]{2,1,0:T(8,128)S(1)}, u32[]{:S(2)}, u32[]{:S(2)}) collective-permute-start(f32[8,32,128]{2,1,0:T(8,128)S(1)} %get-tuple-element.41), channel_id=1, source_target_pairs={{0,2},{1,3},{2,0},{3,1},{4,6},{5,7},{6,4},{7,5},{8,10},{9,11},{10,... | collective-permute-start | bytes 393224 | tf_op jit(solution)/shard_map/ppermute | solution.py:30
  73.9 0.6 collective-permute-start.24
  74.5 3.4 %collective-permute-done.22.b = f32[8,32,128]{2,1,0:T(8,128)S(1)} collective-permute-done((f32[8,32,128]{2,1,0:T(8,128)S(1)}, f32[8,32,128]{2,1,0:T(8,128)S(1)}, u32[]{:S(2)}, u32[]{:S(2)}) %collective-permute-start.22) | collective-permute-done | bytes 131104 | tf_op jit(solution)/shard_map/ppermute | solution.py:30
  77.9 2.3 %collective-permute-done.23.c = f32[8,32,128]{2,1,0:T(8,128)S(1)} collective-permute-done((f32[8,32,128]{2,1,0:T(8,128)S(1)}, f32[8,32,128]{2,1,0:T(8,128)S(1)}, u32[]{:S(2)}, u32[]{:S(2)}) %collective-permute-start.23) | collective-permute-done | bytes 131104 | tf_op jit(solution)/shard_map/ppermute | solution.py:30
  80.2 0.6 collective-permute-done.24.d
  80.8 0.7 shard_map.84
  81.5 3.8 %all-to-all-start.1 = ((f32[8,32,128]{2,1,0:T(8,128)}), f32[8,32,128]{2,1,0:T(8,128)S(1)}, u32[]{:S(2)}, u32[]{:S(2)}) async-start(f32[8,32,128]{2,1,0:T(8,128)} %shard_map.84), calls=%async_computation.1 | async-start | bytes 262144 | tf_op jit(solution)/shard_map/all_to_all | solution.py:306
  85.3 0.3 shard_map.85
  85.6 7.6 %all-to-all-done.1.packed = f32[8,32,128]{2,1,0:T(8,128)S(1)} async-done(((f32[8,32,128]{2,1,0:T(8,128)}), f32[8,32,128]{2,1,0:T(8,128)S(1)}, u32[]{:S(2)}, u32[]{:S(2)}) %all-to-all-start.1) | async-done | bytes 131104 | tf_op jit(solution)/shard_map/all_to_all | solution.py:306
  93.2 1.1 %shard_map.86 = f32[64,512]{1,0:T(8,128)} custom-call(f32[8,32,128]{2,1,0:T(8,128)S(1)} %all-to-all-done.1.packed, bf16[512,512]{1,0:T(8,128)(2,1)S(1)} %get-tuple-element.45.y_high, bf16[512,512]{1,0:T(8,128)(2,1)S(1)} %get-tuple-element.46.y_low), custom_call_target="tpu_custom_call" | custom-call | flops 100663296 | bytes 1310720 | tf_op jit(solution)/shard_map/pallas_call | solution.py:219
  (34 shorter events, 0.2 us)
Async XLA Ops:
  0.0 11.7 %collective-permute-start.3 = (f32[64,1024]{1,0:T(8,128)}, f32[64,1024]{1,0:T(8,128)S(1)}, u32[]{:S(2)}, u32[]{:S(2)}) collective-permute-start(f32[64,1024]{1,0:T(8,128)} %refs_0_.1), channel_id=1, source_target_pairs={{0,224},{32,0},{64,32},{96,64},{128,96},{160,128},{192,160},{224,1... | collective-permute-start | bytes 786440 | tf_op jit(solution)/shard_map/ppermute | solution.py:30
  6.4 8.6 %collective-permute-start = (f32[64,1024]{1,0:T(8,128)}, f32[64,1024]{1,0:T(8,128)S(1)}, u32[]{:S(2)}, u32[]{:S(2)}) collective-permute-start(f32[64,1024]{1,0:T(8,128)} %refs_0_.1), channel_id=1, source_target_pairs={{0,32},{32,64},{64,96},{96,128},{128,160},{160,192},{192,224},{224... | collective-permute-start | bytes 786440 | tf_op jit(solution)/shard_map/ppermute | solution.py:30
  11.7 9.7 %collective-permute-start.4 = (f32[64,1024]{1,0:T(8,128)S(1)}, f32[64,1024]{1,0:T(8,128)S(1)}, u32[]{:S(2)}, u32[]{:S(2)}) collective-permute-start(f32[64,1024]{1,0:T(8,128)S(1)} %collective-permute-done.3.refs_4_), channel_id=1, source_target_pairs={{0,224},{32,0},{64,32},{96,64},{128,96},{160,128},{192,160},{224,1... | collective-permute-start | bytes 786440 | tf_op jit(solution)/shard_map/ppermute | solution.py:30
  15.0 9.1 %collective-permute-start.1 = (f32[64,1024]{1,0:T(8,128)S(1)}, f32[64,1024]{1,0:T(8,128)S(1)}, u32[]{:S(2)}, u32[]{:S(2)}) collective-permute-start(f32[64,1024]{1,0:T(8,128)S(1)} %collective-permute-done.refs_1_), channel_id=1, source_target_pairs={{0,32},{32,64},{64,96},{96,128},{128,160},{160,192},{192,224},{224... | collective-permute-start | bytes 786440 | tf_op jit(solution)/shard_map/ppermute | solution.py:30
  17.4 12.0 %all-to-all-start = ((f32[8,32,128]{2,1,0:T(8,128)}), f32[8,32,128]{2,1,0:T(8,128)S(1)}, u32[]{:S(2)}, u32[]{:S(2)}) async-start(f32[8,32,128]{2,1,0:T(8,128)} %get-tuple-element.26), calls=%async_computation | async-start | bytes 262144 | tf_op jit(solution)/shard_map/all_to_all | solution.py:246
  21.4 13.1 %collective-permute-start.5 = (f32[64,1024]{1,0:T(8,128)S(1)}, f32[64,1024]{1,0:T(8,128)S(1)}, u32[]{:S(2)}, u32[]{:S(2)}) collective-permute-start(f32[64,1024]{1,0:T(8,128)S(1)} %collective-permute-done.4.refs_5_), channel_id=1, source_target_pairs={{0,224},{32,0},{64,32},{96,64},{128,96},{160,128},{192,160},{224,1... | collective-permute-start | bytes 786440 | tf_op jit(solution)/shard_map/ppermute | solution.py:30
  24.1 10.5 %collective-permute-start.2 = (f32[64,1024]{1,0:T(8,128)S(1)}, f32[64,1024]{1,0:T(8,128)S(1)}, u32[]{:S(2)}, u32[]{:S(2)}) collective-permute-start(f32[64,1024]{1,0:T(8,128)S(1)} %collective-permute-done.1.refs_2_), channel_id=1, source_target_pairs={{0,32},{32,64},{64,96},{96,128},{128,160},{160,192},{192,224},{224... | collective-permute-start | bytes 786440 | tf_op jit(solution)/shard_map/ppermute | solution.py:30
  29.5 6.7 %collective-permute-start.6 = (f32[8,32,128]{2,1,0:T(8,128)S(1)}, f32[8,32,128]{2,1,0:T(8,128)S(1)}, u32[]{:S(2)}, u32[]{:S(2)}) collective-permute-start(f32[8,32,128]{2,1,0:T(8,128)S(1)} %all-to-all-done.refs_7_), channel_id=1, source_target_pairs={{0,1},{1,2},{2,3},{3,0},{4,5},{5,6},{6,7},{7,4},{8,9},{9,10},{10,1... | collective-permute-start | bytes 393224 | tf_op jit(solution)/shard_map/ppermute | solution.py:30
  30.8 6.4 %collective-permute-start.7 = (f32[8,32,128]{2,1,0:T(8,128)S(1)}, f32[8,32,128]{2,1,0:T(8,128)S(1)}, u32[]{:S(2)}, u32[]{:S(2)}) collective-permute-start(f32[8,32,128]{2,1,0:T(8,128)S(1)} %all-to-all-done.refs_7_), channel_id=1, source_target_pairs={{0,2},{1,3},{2,0},{3,1},{4,6},{5,7},{6,4},{7,5},{8,10},{9,11},{10,... | collective-permute-start | bytes 393224 | tf_op jit(solution)/shard_map/ppermute | solution.py:30
  33.4 3.8 %collective-permute-start.8 = (f32[8,32,128]{2,1,0:T(8,128)S(1)}, f32[8,32,128]{2,1,0:T(8,128)S(1)}, u32[]{:S(2)}, u32[]{:S(2)}) collective-permute-start(f32[8,32,128]{2,1,0:T(8,128)S(1)} %all-to-all-done.refs_7_), channel_id=1, source_target_pairs={{0,3},{1,0},{2,1},{3,2},{4,7},{5,4},{6,5},{7,6},{8,11},{9,8},{10,9... | collective-permute-start | bytes 393224 | tf_op jit(solution)/shard_map/ppermute | solution.py:30
  34.5 2.7 %copy-start.4 = (f32[4,4]{1,0:T(4,128)S(1)}, f32[4,4]{1,0:T(4,128)}, u32[]{:S(2)}) copy-start(f32[4,4]{1,0:T(4,128)} %x_vectors.3) | copy-start | bytes 196
  34.5 2.7 %copy-start.6 = (f32[64,1024]{1,0:T(8,128)S(1)}, f32[64,1024]{1,0:T(8,128)}, u32[]{:S(2)}) copy-start(f32[64,1024]{1,0:T(8,128)} %refs_0_.1) | copy-start | bytes 786436
  34.5 4.6 %collective-permute-start.10 = (f32[32,1024]{1,0:T(8,128)S(1)}, f32[32,1024]{1,0:T(8,128)S(1)}, u32[]{:S(2)}, u32[]{:S(2)}) collective-permute-start(f32[32,1024]{1,0:T(8,128)S(1)} %shard_map.76), channel_id=1, source_target_pairs={{0,224},{32,0},{64,32},{96,64},{128,96},{160,128},{192,160},{224,1... | collective-permute-start | bytes 393224 | tf_op jit(solution)/shard_map/ppermute | solution.py:30
  34.6 5.1 %collective-permute-start.9 = (f32[32,1024]{1,0:T(8,128)S(1)}, f32[32,1024]{1,0:T(8,128)S(1)}, u32[]{:S(2)}, u32[]{:S(2)}) collective-permute-start(f32[32,1024]{1,0:T(8,128)S(1)} %shard_map.75), channel_id=1, source_target_pairs={{0,32},{32,64},{64,96},{96,128},{128,160},{160,192},{192,224},{224... | collective-permute-start | bytes 393224 | tf_op jit(solution)/shard_map/ppermute | solution.py:30
  40.1 7.8 %collective-permute-start.11 = (f32[256,512]{1,0:T(8,128)S(1)}, f32[256,512]{1,0:T(8,128)S(1)}, u32[]{:S(2)}, u32[]{:S(2)}) collective-permute-start(f32[256,512]{1,0:T(8,128)S(1)} %get-tuple-element.34), channel_id=1, source_target_pairs={{0,4},{4,0},{1,5},{5,1},{2,6},{6,2},{3,7},{7,3},{8,12},{12,8},{9,1... | collective-permute-start | bytes 1572872 | tf_op jit(solution)/shard_map/ppermute | solution.py:30
  48.0 5.0 %copy-start.2 = (f32[4096]{0:T(1024)S(1)}, f32[4096]{0:T(1024)}, u32[]{:S(2)}) copy-start(f32[4096]{0:T(1024)} %param.11) | copy-start | bytes 49156
  48.1 6.2 %collective-permute-start.12 = (f32[256,128]{1,0:T(8,128)S(1)}, f32[256,128]{1,0:T(8,128)S(1)}, u32[]{:S(2)}, u32[]{:S(2)}) collective-permute-start(f32[256,128]{1,0:T(8,128)S(1)} %get-tuple-element.36), channel_id=1, source_target_pairs={{0,8},{8,16},{16,24},{24,0},{1,9},{9,17},{17,25},{25,1},{2,10},{10... | collective-permute-start | bytes 393224 | tf_op jit(solution)/shard_map/ppermute | solution.py:30
  49.4 8.5 %collective-permute-start.13 = (f32[256,128]{1,0:T(8,128)S(1)}, f32[256,128]{1,0:T(8,128)S(1)}, u32[]{:S(2)}, u32[]{:S(2)}) collective-permute-start(f32[256,128]{1,0:T(8,128)S(1)} %get-tuple-element.37), channel_id=1, source_target_pairs={{0,16},{8,24},{16,0},{24,8},{1,17},{9,25},{17,1},{25,9},{2,18},{10... | collective-permute-start | bytes 393224 | tf_op jit(solution)/shard_map/ppermute | solution.py:30
  51.9 1.2 %copy-start.3 = (f32[512]{0:T(512)S(1)}, f32[512]{0:T(512)}, u32[]{:S(2)}) copy-start(f32[512]{0:T(512)} %param.13) | copy-start | bytes 6148
  51.9 6.0 %collective-permute-start.14 = (f32[256,128]{1,0:T(8,128)S(1)}, f32[256,128]{1,0:T(8,128)S(1)}, u32[]{:S(2)}, u32[]{:S(2)}) collective-permute-start(f32[256,128]{1,0:T(8,128)S(1)} %get-tuple-element.38), channel_id=1, source_target_pairs={{0,24},{8,0},{16,8},{24,16},{1,25},{9,1},{17,9},{25,17},{2,26},{10... | collective-permute-start | bytes 393224 | tf_op jit(solution)/shard_map/ppermute | solution.py:30
  53.0 0.7 copy-start.5
  57.9 6.6 %collective-permute-start.15 = (f32[256,128]{1,0:T(8,128)S(1)}, f32[256,128]{1,0:T(8,128)S(1)}, u32[]{:S(2)}, u32[]{:S(2)}) collective-permute-start(f32[256,128]{1,0:T(8,128)S(1)} %shard_map.81.refs_0_), channel_id=1, source_target_pairs={{0,8},{8,16},{16,24},{24,0},{1,9},{9,17},{17,25},{25,1},{2,10},{10... | collective-permute-start | bytes 393224 | tf_op jit(solution)/shard_map/ppermute | solution.py:30
  59.3 7.2 %collective-permute-start.16 = (f32[256,128]{1,0:T(8,128)S(1)}, f32[256,128]{1,0:T(8,128)S(1)}, u32[]{:S(2)}, u32[]{:S(2)}) collective-permute-start(f32[256,128]{1,0:T(8,128)S(1)} %shard_map.81.refs_0_), channel_id=1, source_target_pairs={{0,16},{8,24},{16,0},{24,8},{1,17},{9,25},{17,1},{25,9},{2,18},{10... | collective-permute-start | bytes 393224 | tf_op jit(solution)/shard_map/ppermute | solution.py:30
  61.4 7.3 %collective-permute-start.17 = (f32[256,128]{1,0:T(8,128)S(1)}, f32[256,128]{1,0:T(8,128)S(1)}, u32[]{:S(2)}, u32[]{:S(2)}) collective-permute-start(f32[256,128]{1,0:T(8,128)S(1)} %shard_map.81.refs_0_), channel_id=1, source_target_pairs={{0,24},{8,0},{16,8},{24,16},{1,25},{9,1},{17,9},{25,17},{2,26},{10... | collective-permute-start | bytes 393224 | tf_op jit(solution)/shard_map/ppermute | solution.py:30
  62.2 7.2 %collective-permute-start.18 = (f32[256,128]{1,0:T(8,128)S(1)}, f32[256,128]{1,0:T(8,128)S(1)}, u32[]{:S(2)}, u32[]{:S(2)}) collective-permute-start(f32[256,128]{1,0:T(8,128)S(1)} %shard_map.81.refs_0_), channel_id=1, source_target_pairs={{0,4},{4,0},{1,5},{5,1},{2,6},{6,2},{3,7},{7,3},{8,12},{12,8},{9,1... | collective-permute-start | bytes 393224 | tf_op jit(solution)/shard_map/ppermute | solution.py:30
  64.5 4.9 %collective-permute-start.19 = (f32[256,128]{1,0:T(8,128)S(1)}, f32[256,128]{1,0:T(8,128)S(1)}, u32[]{:S(2)}, u32[]{:S(2)}) collective-permute-start(f32[256,128]{1,0:T(8,128)S(1)} %collective-permute-done.15.refs_1_), channel_id=1, source_target_pairs={{0,4},{4,0},{1,5},{5,1},{2,6},{6,2},{3,7},{7,3},{8,12},{12,8},{9,1... | collective-permute-start | bytes 393224 | tf_op jit(solution)/shard_map/ppermute | solution.py:30
  66.5 3.1 %collective-permute-start.20 = (f32[256,128]{1,0:T(8,128)S(1)}, f32[256,128]{1,0:T(8,128)S(1)}, u32[]{:S(2)}, u32[]{:S(2)}) collective-permute-start(f32[256,128]{1,0:T(8,128)S(1)} %collective-permute-done.16.refs_2_), channel_id=1, source_target_pairs={{0,4},{4,0},{1,5},{5,1},{2,6},{6,2},{3,7},{7,3},{8,12},{12,8},{9,1... | collective-permute-start | bytes 393224 | tf_op jit(solution)/shard_map/ppermute | solution.py:30
  68.7 1.3 %collective-permute-start.21 = (f32[256,128]{1,0:T(8,128)S(1)}, f32[256,128]{1,0:T(8,128)S(1)}, u32[]{:S(2)}, u32[]{:S(2)}) collective-permute-start(f32[256,128]{1,0:T(8,128)S(1)} %collective-permute-done.17.refs_3_), channel_id=1, source_target_pairs={{0,4},{4,0},{1,5},{5,1},{2,6},{6,2},{3,7},{7,3},{8,12},{12,8},{9,1... | collective-permute-start | bytes 393224 | tf_op jit(solution)/shard_map/ppermute | solution.py:30
  70.0 15.3 %copy-start.1 = (bf16[512,512]{1,0:T(8,128)(2,1)S(1)}, bf16[512,512]{1,0:T(8,128)(2,1)}, u32[]{:S(2)}) copy-start(bf16[512,512]{1,0:T(8,128)(2,1)} %get-tuple-element.44.low) | copy-start | bytes 1572868
  71.5 13.8 %copy-start = (bf16[512,512]{1,0:T(8,128)(2,1)S(1)}, bf16[512,512]{1,0:T(8,128)(2,1)}, u32[]{:S(2)}) copy-start(bf16[512,512]{1,0:T(8,128)(2,1)} %get-tuple-element.43.high) | copy-start | bytes 1572868
  71.5 6.4 %collective-permute-start.22 = (f32[8,32,128]{2,1,0:T(8,128)S(1)}, f32[8,32,128]{2,1,0:T(8,128)S(1)}, u32[]{:S(2)}, u32[]{:S(2)}) collective-permute-start(f32[8,32,128]{2,1,0:T(8,128)S(1)} %get-tuple-element.40), channel_id=1, source_target_pairs={{0,1},{1,2},{2,3},{3,0},{4,5},{5,6},{6,7},{7,4},{8,9},{9,10},{10,1... | collective-permute-start | bytes 393224 | tf_op jit(solution)/shard_map/ppermute | solution.py:30
  71.9 8.2 %collective-permute-start.23 = (f32[8,32,128]{2,1,0:T(8,128)S(1)}, f32[8,32,128]{2,1,0:T(8,128)S(1)}, u32[]{:S(2)}, u32[]{:S(2)}) collective-permute-start(f32[8,32,128]{2,1,0:T(8,128)S(1)} %get-tuple-element.41), channel_id=1, source_target_pairs={{0,2},{1,3},{2,0},{3,1},{4,6},{5,7},{6,4},{7,5},{8,10},{9,11},{10,... | collective-permute-start | bytes 393224 | tf_op jit(solution)/shard_map/ppermute | solution.py:30
  73.9 6.8 %collective-permute-start.24 = (f32[8,32,128]{2,1,0:T(8,128)S(1)}, f32[8,32,128]{2,1,0:T(8,128)S(1)}, u32[]{:S(2)}, u32[]{:S(2)}) collective-permute-start(f32[8,32,128]{2,1,0:T(8,128)S(1)} %get-tuple-element.42), channel_id=1, source_target_pairs={{0,3},{1,0},{2,1},{3,2},{4,7},{5,4},{6,5},{7,6},{8,11},{9,8},{10,9... | collective-permute-start | bytes 393224 | tf_op jit(solution)/shard_map/ppermute | solution.py:30
  81.5 11.8 %all-to-all-start.1 = ((f32[8,32,128]{2,1,0:T(8,128)}), f32[8,32,128]{2,1,0:T(8,128)S(1)}, u32[]{:S(2)}, u32[]{:S(2)}) async-start(f32[8,32,128]{2,1,0:T(8,128)} %shard_map.84), calls=%async_computation.1 | async-start | bytes 262144 | tf_op jit(solution)/shard_map/all_to_all | solution.py:306

commit v3 on v2

--- a/solution.py
+++ b/solution.py
@@ -106,8 +106,8 @@
     low_out[...] = low[...].T
 
 
-def half_kernel(first, came, out):
-    out[...] = came[first : first + 32]
+def part_kernel(first, came, out):
+    out[...] = came[first : first + out.shape[0]]
 
 
 def forward_kernel(x_vectors, *refs):
@@ -146,8 +146,8 @@
 
 
 def to_partner_kernel(partial, field_high, field_low, top, bottom, out, far_high, far_low):
-    far_high[:32], far_low[:32] = two_parts(top[...])
-    far_high[32:], far_low[32:] = two_parts(bottom[...])
+    far_high[:48], far_low[:48] = two_parts(top[...])
+    far_high[48:], far_low[48:] = two_parts(bottom[...])
     far_added(partial, field_high, field_low, far_high, far_low, 1 - lax.axis_index("core"), out)
 
 
@@ -255,8 +255,8 @@
     right2, left2 = shifted(right1, "z", 1), shifted(left1, "z", -1)
     planes = [plane] + [shifted(plane, "y", s) for s in (1, 2, 3)]
     right3, left3 = shifted(right2, "z", 1), shifted(left2, "z", -1)
-    top = call(functools.partial(half_kernel, 0), f32(32, 1024), (right3,), vmem=1 << 20)
-    bottom = call(functools.partial(half_kernel, 32), f32(32, 1024), (left3,), vmem=1 << 20)
+    top = call(functools.partial(part_kernel, 0), f32(48, 1024), (right3,), vmem=1 << 20)
+    bottom = call(functools.partial(part_kernel, 48), f32(16, 1024), (left3,), vmem=1 << 20)
     top, bottom = shifted(top, "z", 1), shifted(bottom, "z", -1)
 
     partial, z_high, z_low, field_high, field_low = call(

time: 95.6 us -> 102 us (1.067)
  waiting for transfers between devices: 31.6 us -> 37.2 us
    ppermute x25, waiting for transfers between devices: 18.6 us -> 24.4 us  [shifted(): return lax.ppermute(value, axis, [(i, (i + step) % n) for i in range(n)])]
    all_to_all x1, starting transfers between devices: 3.96 us -> 5.02 us  [shards(): plane = lax.all_to_all(packed, 'z', 0, 0, tiled=True)]
  transfers between devices with their start and end apart: 27 -> 27, of which waited for: 13 -> 12; matrix products, arithmetic and copies ran while one was open for 0% -> 0% of each run, Pallas kernels for 7% -> 6%
where the time goes in v3:
time: 102 us; the launch traced here: 101 us
  starting transfers between devices  52.5 us (51%)
  waiting for transfers between devices  37.2 us (36%)
  Pallas kernels  10.1 us (10%)
    ppermute x25, starting transfers between devices, shifted(): return lax.ppermute(value, axis, [(i, (i + step) % n) for i in range(n)])  44.1 us
    ppermute x25, waiting for transfers between devices, shifted(): return lax.ppermute(value, axis, [(i, (i + step) % n) for i in range(n)])  24.4 us
    pallas_call x14, Pallas kernels, call(): pl.pallas_call(kernel, out_shape=out_shape, in_specs=[SMEM] * smem + [hel...  10.1 us
    all_to_all x1, waiting for transfers between devices, shards(): back = lax.all_to_all(mine, 'z', 0, 0, tiled=True)  7.59 us
    all_to_all x1, waiting for transfers between devices, shards(): plane = lax.all_to_all(packed, 'z', 0, 0, tiled=True)  5.26 us
    all_to_all x1, starting transfers between devices, shards(): plane = lax.all_to_all(packed, 'z', 0, 0, tiled=True)  5.02 us
    all_to_all x1, starting transfers between devices, shards(): back = lax.all_to_all(mine, 'z', 0, 0, tiled=True)  3.37 us
  transfers between devices with their start and end apart: 27, of which 12 were waited for; matrix products, arithmetic and copies ran while one was open for 0% of the time, Pallas kernels for 6%

profile of v3, /device:TPU:1, one launch (start us, length us, event | category | flops | bytes accessed | tf_op | source)
XLA Modules:
  0.0 100.6 jit_solution(14228644799864398787)
XLA Ops:
  0.0 2.5 %collective-permute-start = (f32[64,1024]{1,0:T(8,128)}, f32[64,1024]{1,0:T(8,128)S(1)}, u32[]{:S(2)}, u32[]{:S(2)}) collective-permute-start(f32[64,1024]{1,0:T(8,128)} %refs_0_.1), channel_id=1, source_target_pairs={{0,32},{32,64},{64,96},{96,128},{128,160},{160,192},{192,224},{224... | collective-permute-start | bytes 786440 | tf_op jit(solution)/shard_map/ppermute | solution.py:30
  2.5 3.9 %collective-permute-start.3 = (f32[64,1024]{1,0:T(8,128)}, f32[64,1024]{1,0:T(8,128)S(1)}, u32[]{:S(2)}, u32[]{:S(2)}) collective-permute-start(f32[64,1024]{1,0:T(8,128)} %refs_0_.1), channel_id=1, source_target_pairs={{0,224},{32,0},{64,32},{96,64},{128,96},{160,128},{192,160},{224,1... | collective-permute-start | bytes 786440 | tf_op jit(solution)/shard_map/ppermute | solution.py:30
  6.4 6.2 %collective-permute-done.refs_1_ = f32[64,1024]{1,0:T(8,128)S(1)} collective-permute-done((f32[64,1024]{1,0:T(8,128)}, f32[64,1024]{1,0:T(8,128)S(1)}, u32[]{:S(2)}, u32[]{:S(2)}) %collective-permute-start) | collective-permute-done | bytes 262176 | tf_op jit(solution)/shard_map/ppermute | solution.py:30
  12.6 2.7 %collective-permute-start.4 = (f32[64,1024]{1,0:T(8,128)S(1)}, f32[64,1024]{1,0:T(8,128)S(1)}, u32[]{:S(2)}, u32[]{:S(2)}) collective-permute-start(f32[64,1024]{1,0:T(8,128)S(1)} %collective-permute-done.3.refs_4_), channel_id=1, source_target_pairs={{0,224},{32,0},{64,32},{96,64},{128,96},{160,128},{192,160},{224,1... | collective-permute-start | bytes 786440 | tf_op jit(solution)/shard_map/ppermute | solution.py:30
  15.3 5.1 %collective-permute-done.1.refs_2_ = f32[64,1024]{1,0:T(8,128)S(1)} collective-permute-done((f32[64,1024]{1,0:T(8,128)S(1)}, f32[64,1024]{1,0:T(8,128)S(1)}, u32[]{:S(2)}, u32[]{:S(2)}) %collective-permute-start.1) | collective-permute-done | bytes 262176 | tf_op jit(solution)/shard_map/ppermute | solution.py:30
  20.4 2.4 %shard_map.73 = (f32[8,32,128]{2,1,0:T(8,128)}, bf16[512,512]{1,0:T(8,128)(2,1)}, bf16[512,512]{1,0:T(8,128)(2,1)}) custom-call(f32[64,512]{1,0:T(8,128)} %source.1, f32[512,512]{1,0:T(8,128)} %y_vectors.1), custom_call_target="tpu_custom_call" | custom-call | flops 100663296 | bytes 2359296 | tf_op jit(solution)/shard_map/pallas_call | solution.py:219
  22.9 5.0 %all-to-all-start = ((f32[8,32,128]{2,1,0:T(8,128)}), f32[8,32,128]{2,1,0:T(8,128)S(1)}, u32[]{:S(2)}, u32[]{:S(2)}) async-start(f32[8,32,128]{2,1,0:T(8,128)} %get-tuple-element.26), calls=%async_computation | async-start | bytes 262144 | tf_op jit(solution)/shard_map/all_to_all | solution.py:246
  27.9 2.7 %collective-permute-start.5 = (f32[64,1024]{1,0:T(8,128)S(1)}, f32[64,1024]{1,0:T(8,128)S(1)}, u32[]{:S(2)}, u32[]{:S(2)}) collective-permute-start(f32[64,1024]{1,0:T(8,128)S(1)} %collective-permute-done.4.refs_5_), channel_id=1, source_target_pairs={{0,224},{32,0},{64,32},{96,64},{128,96},{160,128},{192,160},{224,1... | collective-permute-start | bytes 786440 | tf_op jit(solution)/shard_map/ppermute | solution.py:30
  30.6 5.3 %all-to-all-done.refs_7_ = f32[8,32,128]{2,1,0:T(8,128)S(1)} async-done(((f32[8,32,128]{2,1,0:T(8,128)}), f32[8,32,128]{2,1,0:T(8,128)S(1)}, u32[]{:S(2)}, u32[]{:S(2)}) %all-to-all-start) | async-done | bytes 131104 | tf_op jit(solution)/shard_map/all_to_all | solution.py:246
  35.8 1.3 %collective-permute-start.6 = (f32[8,32,128]{2,1,0:T(8,128)S(1)}, f32[8,32,128]{2,1,0:T(8,128)S(1)}, u32[]{:S(2)}, u32[]{:S(2)}) collective-permute-start(f32[8,32,128]{2,1,0:T(8,128)S(1)} %all-to-all-done.refs_7_), channel_id=1, source_target_pairs={{0,1},{1,2},{2,3},{3,0},{4,5},{5,6},{6,7},{7,4},{8,9},{9,10},{10,1... | collective-permute-start | bytes 393224 | tf_op jit(solution)/shard_map/ppermute | solution.py:30
  37.1 2.6 %collective-permute-start.7 = (f32[8,32,128]{2,1,0:T(8,128)S(1)}, f32[8,32,128]{2,1,0:T(8,128)S(1)}, u32[]{:S(2)}, u32[]{:S(2)}) collective-permute-start(f32[8,32,128]{2,1,0:T(8,128)S(1)} %all-to-all-done.refs_7_), channel_id=1, source_target_pairs={{0,2},{1,3},{2,0},{3,1},{4,6},{5,7},{6,4},{7,5},{8,10},{9,11},{10,... | collective-permute-start | bytes 393224 | tf_op jit(solution)/shard_map/ppermute | solution.py:30
  39.7 1.1 %collective-permute-start.8 = (f32[8,32,128]{2,1,0:T(8,128)S(1)}, f32[8,32,128]{2,1,0:T(8,128)S(1)}, u32[]{:S(2)}, u32[]{:S(2)}) collective-permute-start(f32[8,32,128]{2,1,0:T(8,128)S(1)} %all-to-all-done.refs_7_), channel_id=1, source_target_pairs={{0,3},{1,0},{2,1},{3,2},{4,7},{5,4},{6,5},{7,6},{8,11},{9,8},{10,9... | collective-permute-start | bytes 393224 | tf_op jit(solution)/shard_map/ppermute | solution.py:30
  40.9 0.4 collective-permute-start.9
  41.2 2.5 %collective-permute-start.10 = (f32[16,1024]{1,0:T(8,128)S(1)}, f32[16,1024]{1,0:T(8,128)S(1)}, u32[]{:S(2)}, u32[]{:S(2)}) collective-permute-start(f32[16,1024]{1,0:T(8,128)S(1)} %shard_map.76), channel_id=1, source_target_pairs={{0,224},{32,0},{64,32},{96,64},{128,96},{160,128},{192,160},{224,1... | collective-permute-start | bytes 196616 | tf_op jit(solution)/shard_map/ppermute | solution.py:30
  43.7 1.8 %shard_map.74 = (f32[256,1024]{1,0:T(8,128)S(1)}, bf16[512,1024]{1,0:T(8,128)(2,1)S(1)}, bf16[512,1024]{1,0:T(8,128)(2,1)S(1)}, bf16[256,128]{1,0:T(8,128)(2,1)S(1)}, bf16[256,128]{1,0:T(8,128)(2,1)S(1)}) custom-call(f32[4,4]{1,0:T(4,128)S(1)} %copy-done.4, f32[64,1024]{1,0:T(8,128)S(1)} %copy-done.6, f32[64,1024]{1,0:T(8,128)S(1)} %collective-permute-done.refs_1_, ...), custom_call_target="tpu_custom_call" | custom-call | flops 805306368 | bytes 5636160 | tf_op jit(solution)/shard_map/pallas_call | solution.py:219
  45.6 1.4 %collective-permute-done.9.top = f32[48,1024]{1,0:T(8,128)S(1)} collective-permute-done((f32[48,1024]{1,0:T(8,128)S(1)}, f32[48,1024]{1,0:T(8,128)S(1)}, u32[]{:S(2)}, u32[]{:S(2)}) %collective-permute-start.9) | collective-permute-done | bytes 196640 | tf_op jit(solution)/shard_map/ppermute | solution.py:30
  47.0 0.4 shard_map.77
  47.4 5.9 %collective-permute-start.11 = (f32[256,512]{1,0:T(8,128)S(1)}, f32[256,512]{1,0:T(8,128)S(1)}, u32[]{:S(2)}, u32[]{:S(2)}) collective-permute-start(f32[256,512]{1,0:T(8,128)S(1)} %get-tuple-element.34), channel_id=1, source_target_pairs={{0,4},{4,0},{1,5},{5,1},{2,6},{6,2},{3,7},{7,3},{8,12},{12,8},{9,1... | collective-permute-start | bytes 1572872 | tf_op jit(solution)/shard_map/ppermute | solution.py:30
  53.2 0.3 shard_map.78.kept
  53.6 1.2 %collective-permute-done.11.received = f32[256,512]{1,0:T(8,128)S(1)} collective-permute-done((f32[256,512]{1,0:T(8,128)S(1)}, f32[256,512]{1,0:T(8,128)S(1)}, u32[]{:S(2)}, u32[]{:S(2)}) %collective-permute-start.11) | collective-permute-done | bytes 524320 | tf_op jit(solution)/shard_map/ppermute | solution.py:30
  54.8 0.1 shard_map.79
  54.9 1.3 %collective-permute-start.12 = (f32[256,128]{1,0:T(8,128)S(1)}, f32[256,128]{1,0:T(8,128)S(1)}, u32[]{:S(2)}, u32[]{:S(2)}) collective-permute-start(f32[256,128]{1,0:T(8,128)S(1)} %get-tuple-element.36), channel_id=1, source_target_pairs={{0,8},{8,16},{16,24},{24,0},{1,9},{9,17},{17,25},{25,1},{2,10},{10... | collective-permute-start | bytes 393224 | tf_op jit(solution)/shard_map/ppermute | solution.py:30
  56.2 2.4 %collective-permute-start.13 = (f32[256,128]{1,0:T(8,128)S(1)}, f32[256,128]{1,0:T(8,128)S(1)}, u32[]{:S(2)}, u32[]{:S(2)}) collective-permute-start(f32[256,128]{1,0:T(8,128)S(1)} %get-tuple-element.37), channel_id=1, source_target_pairs={{0,16},{8,24},{16,0},{24,8},{1,17},{9,25},{17,1},{25,9},{2,18},{10... | collective-permute-start | bytes 393224 | tf_op jit(solution)/shard_map/ppermute | solution.py:30
  58.6 1.2 %collective-permute-start.14 = (f32[256,128]{1,0:T(8,128)S(1)}, f32[256,128]{1,0:T(8,128)S(1)}, u32[]{:S(2)}, u32[]{:S(2)}) collective-permute-start(f32[256,128]{1,0:T(8,128)S(1)} %get-tuple-element.38), channel_id=1, source_target_pairs={{0,24},{8,0},{16,8},{24,16},{1,25},{9,1},{17,9},{25,17},{2,26},{10... | collective-permute-start | bytes 393224 | tf_op jit(solution)/shard_map/ppermute | solution.py:30
  59.8 0.6 copy-done.5
  60.5 0.7 shard_map.80.divisor
  61.1 3.5 %collective-permute-done.13.c = f32[256,128]{1,0:T(8,128)S(1)} collective-permute-done((f32[256,128]{1,0:T(8,128)S(1)}, f32[256,128]{1,0:T(8,128)S(1)}, u32[]{:S(2)}, u32[]{:S(2)}) %collective-permute-start.13) | collective-permute-done | bytes 131104 | tf_op jit(solution)/shard_map/ppermute | solution.py:30
  64.7 1.4 %collective-permute-start.15 = (f32[256,128]{1,0:T(8,128)S(1)}, f32[256,128]{1,0:T(8,128)S(1)}, u32[]{:S(2)}, u32[]{:S(2)}) collective-permute-start(f32[256,128]{1,0:T(8,128)S(1)} %shard_map.81.refs_0_), channel_id=1, source_target_pairs={{0,8},{8,16},{16,24},{24,0},{1,9},{9,17},{17,25},{25,1},{2,10},{10... | collective-permute-start | bytes 393224 | tf_op jit(solution)/shard_map/ppermute | solution.py:30
  66.1 2.1 %collective-permute-start.16 = (f32[256,128]{1,0:T(8,128)S(1)}, f32[256,128]{1,0:T(8,128)S(1)}, u32[]{:S(2)}, u32[]{:S(2)}) collective-permute-start(f32[256,128]{1,0:T(8,128)S(1)} %shard_map.81.refs_0_), channel_id=1, source_target_pairs={{0,16},{8,24},{16,0},{24,8},{1,17},{9,25},{17,1},{25,9},{2,18},{10... | collective-permute-start | bytes 393224 | tf_op jit(solution)/shard_map/ppermute | solution.py:30
  68.2 0.8 collective-permute-start.17
  69.0 2.3 %collective-permute-start.18 = (f32[256,128]{1,0:T(8,128)S(1)}, f32[256,128]{1,0:T(8,128)S(1)}, u32[]{:S(2)}, u32[]{:S(2)}) collective-permute-start(f32[256,128]{1,0:T(8,128)S(1)} %shard_map.81.refs_0_), channel_id=1, source_target_pairs={{0,4},{4,0},{1,5},{5,1},{2,6},{6,2},{3,7},{7,3},{8,12},{12,8},{9,1... | collective-permute-start | bytes 393224 | tf_op jit(solution)/shard_map/ppermute | solution.py:30
  71.3 2.0 %collective-permute-start.19 = (f32[256,128]{1,0:T(8,128)S(1)}, f32[256,128]{1,0:T(8,128)S(1)}, u32[]{:S(2)}, u32[]{:S(2)}) collective-permute-start(f32[256,128]{1,0:T(8,128)S(1)} %collective-permute-done.15.refs_1_), channel_id=1, source_target_pairs={{0,4},{4,0},{1,5},{5,1},{2,6},{6,2},{3,7},{7,3},{8,12},{12,8},{9,1... | collective-permute-start | bytes 393224 | tf_op jit(solution)/shard_map/ppermute | solution.py:30
  73.3 2.1 %collective-permute-start.20 = (f32[256,128]{1,0:T(8,128)S(1)}, f32[256,128]{1,0:T(8,128)S(1)}, u32[]{:S(2)}, u32[]{:S(2)}) collective-permute-start(f32[256,128]{1,0:T(8,128)S(1)} %collective-permute-done.16.refs_2_), channel_id=1, source_target_pairs={{0,4},{4,0},{1,5},{5,1},{2,6},{6,2},{3,7},{7,3},{8,12},{12,8},{9,1... | collective-permute-start | bytes 393224 | tf_op jit(solution)/shard_map/ppermute | solution.py:30
  75.5 0.7 shard_map.82.own
  76.2 0.2 collective-permute-done.20.refs_2_
  76.4 0.4 collective-permute-done.21.refs_3_
  76.8 1.4 %shard_map.83 = (f32[8,32,128]{2,1,0:T(8,128)S(1)}, f32[8,32,128]{2,1,0:T(8,128)S(1)}, f32[8,32,128]{2,1,0:T(8,128)S(1)}, f32[8,32,128]{2,1,0:T(8,128)S(1)}) custom-call(f32[4,4]{1,0:T(4,128)S(1)} %copy-done.4, f32[512,256]{1,0:T(8,128)S(1)} %shard_map.82.own, bf16[512,1024]{1,0:T(8,128)(2,1)S(1)} %get-tuple-element.27.z_high, ...), custom_call_target="tpu_custom_call" | custom-call | flops 402653184 | bytes 3932224 | tf_op jit(solution)/shard_map/pallas_call | solution.py:219
  78.2 0.5 collective-permute-start.22
  78.7 1.6 %collective-permute-start.23 = (f32[8,32,128]{2,1,0:T(8,128)S(1)}, f32[8,32,128]{2,1,0:T(8,128)S(1)}, u32[]{:S(2)}, u32[]{:S(2)}) collective-permute-start(f32[8,32,128]{2,1,0:T(8,128)S(1)} %get-tuple-element.41), channel_id=1, source_target_pairs={{0,2},{1,3},{2,0},{3,1},{4,6},{5,7},{6,4},{7,5},{8,10},{9,11},{10,... | collective-permute-start | bytes 393224 | tf_op jit(solution)/shard_map/ppermute | solution.py:30
  80.3 0.9 collective-permute-start.24
  81.2 3.8 %collective-permute-done.22.b = f32[8,32,128]{2,1,0:T(8,128)S(1)} collective-permute-done((f32[8,32,128]{2,1,0:T(8,128)S(1)}, f32[8,32,128]{2,1,0:T(8,128)S(1)}, u32[]{:S(2)}, u32[]{:S(2)}) %collective-permute-start.22) | collective-permute-done | bytes 131104 | tf_op jit(solution)/shard_map/ppermute | solution.py:30
  85.1 1.5 %collective-permute-done.23.c = f32[8,32,128]{2,1,0:T(8,128)S(1)} collective-permute-done((f32[8,32,128]{2,1,0:T(8,128)S(1)}, f32[8,32,128]{2,1,0:T(8,128)S(1)}, u32[]{:S(2)}, u32[]{:S(2)}) %collective-permute-start.23) | collective-permute-done | bytes 131104 | tf_op jit(solution)/shard_map/ppermute | solution.py:30
  86.5 1.0 %collective-permute-done.24.d = f32[8,32,128]{2,1,0:T(8,128)S(1)} collective-permute-done((f32[8,32,128]{2,1,0:T(8,128)S(1)}, f32[8,32,128]{2,1,0:T(8,128)S(1)}, u32[]{:S(2)}, u32[]{:S(2)}) %collective-permute-start.24) | collective-permute-done | bytes 131104 | tf_op jit(solution)/shard_map/ppermute | solution.py:30
  87.6 0.7 shard_map.84
  88.2 3.4 %all-to-all-start.1 = ((f32[8,32,128]{2,1,0:T(8,128)}), f32[8,32,128]{2,1,0:T(8,128)S(1)}, u32[]{:S(2)}, u32[]{:S(2)}) async-start(f32[8,32,128]{2,1,0:T(8,128)} %shard_map.84), calls=%async_computation.1 | async-start | bytes 262144 | tf_op jit(solution)/shard_map/all_to_all | solution.py:306
  91.6 0.3 shard_map.85
  92.0 7.6 %all-to-all-done.1.packed = f32[8,32,128]{2,1,0:T(8,128)S(1)} async-done(((f32[8,32,128]{2,1,0:T(8,128)}), f32[8,32,128]{2,1,0:T(8,128)S(1)}, u32[]{:S(2)}, u32[]{:S(2)}) %all-to-all-start.1) | async-done | bytes 131104 | tf_op jit(solution)/shard_map/all_to_all | solution.py:306
  99.6 1.1 %shard_map.86 = f32[64,512]{1,0:T(8,128)} custom-call(f32[8,32,128]{2,1,0:T(8,128)S(1)} %all-to-all-done.1.packed, bf16[512,512]{1,0:T(8,128)(2,1)S(1)} %get-tuple-element.45.y_high, bf16[512,512]{1,0:T(8,128)(2,1)S(1)} %get-tuple-element.46.y_low), custom_call_target="tpu_custom_call" | custom-call | flops 100663296 | bytes 1310720 | tf_op jit(solution)/shard_map/pallas_call | solution.py:219
  (34 shorter events, 0.2 us)
Async XLA Ops:
  0.0 12.6 %collective-permute-start = (f32[64,1024]{1,0:T(8,128)}, f32[64,1024]{1,0:T(8,128)S(1)}, u32[]{:S(2)}, u32[]{:S(2)}) collective-permute-start(f32[64,1024]{1,0:T(8,128)} %refs_0_.1), channel_id=1, source_target_pairs={{0,32},{32,64},{64,96},{96,128},{128,160},{160,192},{192,224},{224... | collective-permute-start | bytes 786440 | tf_op jit(solution)/shard_map/ppermute | solution.py:30
  2.5 10.2 %collective-permute-start.3 = (f32[64,1024]{1,0:T(8,128)}, f32[64,1024]{1,0:T(8,128)S(1)}, u32[]{:S(2)}, u32[]{:S(2)}) collective-permute-start(f32[64,1024]{1,0:T(8,128)} %refs_0_.1), channel_id=1, source_target_pairs={{0,224},{32,0},{64,32},{96,64},{128,96},{160,128},{192,160},{224,1... | collective-permute-start | bytes 786440 | tf_op jit(solution)/shard_map/ppermute | solution.py:30
  12.6 7.8 %collective-permute-start.1 = (f32[64,1024]{1,0:T(8,128)S(1)}, f32[64,1024]{1,0:T(8,128)S(1)}, u32[]{:S(2)}, u32[]{:S(2)}) collective-permute-start(f32[64,1024]{1,0:T(8,128)S(1)} %collective-permute-done.refs_1_), channel_id=1, source_target_pairs={{0,32},{32,64},{64,96},{96,128},{128,160},{160,192},{192,224},{224... | collective-permute-start | bytes 786440 | tf_op jit(solution)/shard_map/ppermute | solution.py:30
  12.6 15.3 %collective-permute-start.4 = (f32[64,1024]{1,0:T(8,128)S(1)}, f32[64,1024]{1,0:T(8,128)S(1)}, u32[]{:S(2)}, u32[]{:S(2)}) collective-permute-start(f32[64,1024]{1,0:T(8,128)S(1)} %collective-permute-done.3.refs_4_), channel_id=1, source_target_pairs={{0,224},{32,0},{64,32},{96,64},{128,96},{160,128},{192,160},{224,1... | collective-permute-start | bytes 786440 | tf_op jit(solution)/shard_map/ppermute | solution.py:30
  20.4 20.4 %collective-permute-start.2 = (f32[64,1024]{1,0:T(8,128)S(1)}, f32[64,1024]{1,0:T(8,128)S(1)}, u32[]{:S(2)}, u32[]{:S(2)}) collective-permute-start(f32[64,1024]{1,0:T(8,128)S(1)} %collective-permute-done.1.refs_2_), channel_id=1, source_target_pairs={{0,32},{32,64},{64,96},{96,128},{128,160},{160,192},{192,224},{224... | collective-permute-start | bytes 786440 | tf_op jit(solution)/shard_map/ppermute | solution.py:30
  22.9 13.0 %all-to-all-start = ((f32[8,32,128]{2,1,0:T(8,128)}), f32[8,32,128]{2,1,0:T(8,128)S(1)}, u32[]{:S(2)}, u32[]{:S(2)}) async-start(f32[8,32,128]{2,1,0:T(8,128)} %get-tuple-element.26), calls=%async_computation | async-start | bytes 262144 | tf_op jit(solution)/shard_map/all_to_all | solution.py:246
  27.9 13.3 %collective-permute-start.5 = (f32[64,1024]{1,0:T(8,128)S(1)}, f32[64,1024]{1,0:T(8,128)S(1)}, u32[]{:S(2)}, u32[]{:S(2)}) collective-permute-start(f32[64,1024]{1,0:T(8,128)S(1)} %collective-permute-done.4.refs_5_), channel_id=1, source_target_pairs={{0,224},{32,0},{64,32},{96,64},{128,96},{160,128},{192,160},{224,1... | collective-permute-start | bytes 786440 | tf_op jit(solution)/shard_map/ppermute | solution.py:30
  35.8 7.9 %collective-permute-start.6 = (f32[8,32,128]{2,1,0:T(8,128)S(1)}, f32[8,32,128]{2,1,0:T(8,128)S(1)}, u32[]{:S(2)}, u32[]{:S(2)}) collective-permute-start(f32[8,32,128]{2,1,0:T(8,128)S(1)} %all-to-all-done.refs_7_), channel_id=1, source_target_pairs={{0,1},{1,2},{2,3},{3,0},{4,5},{5,6},{6,7},{7,4},{8,9},{9,10},{10,1... | collective-permute-start | bytes 393224 | tf_op jit(solution)/shard_map/ppermute | solution.py:30
  37.1 6.6 %collective-permute-start.7 = (f32[8,32,128]{2,1,0:T(8,128)S(1)}, f32[8,32,128]{2,1,0:T(8,128)S(1)}, u32[]{:S(2)}, u32[]{:S(2)}) collective-permute-start(f32[8,32,128]{2,1,0:T(8,128)S(1)} %all-to-all-done.refs_7_), channel_id=1, source_target_pairs={{0,2},{1,3},{2,0},{3,1},{4,6},{5,7},{6,4},{7,5},{8,10},{9,11},{10,... | collective-permute-start | bytes 393224 | tf_op jit(solution)/shard_map/ppermute | solution.py:30
  39.7 4.0 %collective-permute-start.8 = (f32[8,32,128]{2,1,0:T(8,128)S(1)}, f32[8,32,128]{2,1,0:T(8,128)S(1)}, u32[]{:S(2)}, u32[]{:S(2)}) collective-permute-start(f32[8,32,128]{2,1,0:T(8,128)S(1)} %all-to-all-done.refs_7_), channel_id=1, source_target_pairs={{0,3},{1,0},{2,1},{3,2},{4,7},{5,4},{6,5},{7,6},{8,11},{9,8},{10,9... | collective-permute-start | bytes 393224 | tf_op jit(solution)/shard_map/ppermute | solution.py:30
  40.8 2.9 %copy-start.4 = (f32[4,4]{1,0:T(4,128)S(1)}, f32[4,4]{1,0:T(4,128)}, u32[]{:S(2)}) copy-start(f32[4,4]{1,0:T(4,128)} %x_vectors.3) | copy-start | bytes 196
  40.8 2.9 %copy-start.6 = (f32[64,1024]{1,0:T(8,128)S(1)}, f32[64,1024]{1,0:T(8,128)}, u32[]{:S(2)}) copy-start(f32[64,1024]{1,0:T(8,128)} %refs_0_.1) | copy-start | bytes 786436
  40.9 6.1 %collective-permute-start.9 = (f32[48,1024]{1,0:T(8,128)S(1)}, f32[48,1024]{1,0:T(8,128)S(1)}, u32[]{:S(2)}, u32[]{:S(2)}) collective-permute-start(f32[48,1024]{1,0:T(8,128)S(1)} %shard_map.75), channel_id=1, source_target_pairs={{0,32},{32,64},{64,96},{96,128},{128,160},{160,192},{192,224},{224... | collective-permute-start | bytes 589832 | tf_op jit(solution)/shard_map/ppermute | solution.py:30
  41.2 4.4 %collective-permute-start.10 = (f32[16,1024]{1,0:T(8,128)S(1)}, f32[16,1024]{1,0:T(8,128)S(1)}, u32[]{:S(2)}, u32[]{:S(2)}) collective-permute-start(f32[16,1024]{1,0:T(8,128)S(1)} %shard_map.76), channel_id=1, source_target_pairs={{0,224},{32,0},{64,32},{96,64},{128,96},{160,128},{192,160},{224,1... | collective-permute-start | bytes 196616 | tf_op jit(solution)/shard_map/ppermute | solution.py:30
  47.4 7.4 %collective-permute-start.11 = (f32[256,512]{1,0:T(8,128)S(1)}, f32[256,512]{1,0:T(8,128)S(1)}, u32[]{:S(2)}, u32[]{:S(2)}) collective-permute-start(f32[256,512]{1,0:T(8,128)S(1)} %get-tuple-element.34), channel_id=1, source_target_pairs={{0,4},{4,0},{1,5},{5,1},{2,6},{6,2},{3,7},{7,3},{8,12},{12,8},{9,1... | collective-permute-start | bytes 1572872 | tf_op jit(solution)/shard_map/ppermute | solution.py:30
  54.8 5.0 %copy-start.2 = (f32[4096]{0:T(1024)S(1)}, f32[4096]{0:T(1024)}, u32[]{:S(2)}) copy-start(f32[4096]{0:T(1024)} %param.11) | copy-start | bytes 49156
  54.9 6.2 %collective-permute-start.12 = (f32[256,128]{1,0:T(8,128)S(1)}, f32[256,128]{1,0:T(8,128)S(1)}, u32[]{:S(2)}, u32[]{:S(2)}) collective-permute-start(f32[256,128]{1,0:T(8,128)S(1)} %get-tuple-element.36), channel_id=1, source_target_pairs={{0,8},{8,16},{16,24},{24,0},{1,9},{9,17},{17,25},{25,1},{2,10},{10... | collective-permute-start | bytes 393224 | tf_op jit(solution)/shard_map/ppermute | solution.py:30
  56.2 8.5 %collective-permute-start.13 = (f32[256,128]{1,0:T(8,128)S(1)}, f32[256,128]{1,0:T(8,128)S(1)}, u32[]{:S(2)}, u32[]{:S(2)}) collective-permute-start(f32[256,128]{1,0:T(8,128)S(1)} %get-tuple-element.37), channel_id=1, source_target_pairs={{0,16},{8,24},{16,0},{24,8},{1,17},{9,25},{17,1},{25,9},{2,18},{10... | collective-permute-start | bytes 393224 | tf_op jit(solution)/shard_map/ppermute | solution.py:30
  58.6 1.2 %copy-start.3 = (f32[512]{0:T(512)S(1)}, f32[512]{0:T(512)}, u32[]{:S(2)}) copy-start(f32[512]{0:T(512)} %param.13) | copy-start | bytes 6148
  58.6 6.0 %collective-permute-start.14 = (f32[256,128]{1,0:T(8,128)S(1)}, f32[256,128]{1,0:T(8,128)S(1)}, u32[]{:S(2)}, u32[]{:S(2)}) collective-permute-start(f32[256,128]{1,0:T(8,128)S(1)} %get-tuple-element.38), channel_id=1, source_target_pairs={{0,24},{8,0},{16,8},{24,16},{1,25},{9,1},{17,9},{25,17},{2,26},{10... | collective-permute-start | bytes 393224 | tf_op jit(solution)/shard_map/ppermute | solution.py:30
  59.8 0.7 copy-start.5
  64.7 6.6 %collective-permute-start.15 = (f32[256,128]{1,0:T(8,128)S(1)}, f32[256,128]{1,0:T(8,128)S(1)}, u32[]{:S(2)}, u32[]{:S(2)}) collective-permute-start(f32[256,128]{1,0:T(8,128)S(1)} %shard_map.81.refs_0_), channel_id=1, source_target_pairs={{0,8},{8,16},{16,24},{24,0},{1,9},{9,17},{17,25},{25,1},{2,10},{10... | collective-permute-start | bytes 393224 | tf_op jit(solution)/shard_map/ppermute | solution.py:30
  66.1 7.2 %collective-permute-start.16 = (f32[256,128]{1,0:T(8,128)S(1)}, f32[256,128]{1,0:T(8,128)S(1)}, u32[]{:S(2)}, u32[]{:S(2)}) collective-permute-start(f32[256,128]{1,0:T(8,128)S(1)} %shard_map.81.refs_0_), channel_id=1, source_target_pairs={{0,16},{8,24},{16,0},{24,8},{1,17},{9,25},{17,1},{25,9},{2,18},{10... | collective-permute-start | bytes 393224 | tf_op jit(solution)/shard_map/ppermute | solution.py:30
  68.2 7.3 %collective-permute-start.17 = (f32[256,128]{1,0:T(8,128)S(1)}, f32[256,128]{1,0:T(8,128)S(1)}, u32[]{:S(2)}, u32[]{:S(2)}) collective-permute-start(f32[256,128]{1,0:T(8,128)S(1)} %shard_map.81.refs_0_), channel_id=1, source_target_pairs={{0,24},{8,0},{16,8},{24,16},{1,25},{9,1},{17,9},{25,17},{2,26},{10... | collective-permute-start | bytes 393224 | tf_op jit(solution)/shard_map/ppermute | solution.py:30
  69.0 7.2 %collective-permute-start.18 = (f32[256,128]{1,0:T(8,128)S(1)}, f32[256,128]{1,0:T(8,128)S(1)}, u32[]{:S(2)}, u32[]{:S(2)}) collective-permute-start(f32[256,128]{1,0:T(8,128)S(1)} %shard_map.81.refs_0_), channel_id=1, source_target_pairs={{0,4},{4,0},{1,5},{5,1},{2,6},{6,2},{3,7},{7,3},{8,12},{12,8},{9,1... | collective-permute-start | bytes 393224 | tf_op jit(solution)/shard_map/ppermute | solution.py:30
  71.3 4.9 %collective-permute-start.19 = (f32[256,128]{1,0:T(8,128)S(1)}, f32[256,128]{1,0:T(8,128)S(1)}, u32[]{:S(2)}, u32[]{:S(2)}) collective-permute-start(f32[256,128]{1,0:T(8,128)S(1)} %collective-permute-done.15.refs_1_), channel_id=1, source_target_pairs={{0,4},{4,0},{1,5},{5,1},{2,6},{6,2},{3,7},{7,3},{8,12},{12,8},{9,1... | collective-permute-start | bytes 393224 | tf_op jit(solution)/shard_map/ppermute | solution.py:30
  73.3 3.1 %collective-permute-start.20 = (f32[256,128]{1,0:T(8,128)S(1)}, f32[256,128]{1,0:T(8,128)S(1)}, u32[]{:S(2)}, u32[]{:S(2)}) collective-permute-start(f32[256,128]{1,0:T(8,128)S(1)} %collective-permute-done.16.refs_2_), channel_id=1, source_target_pairs={{0,4},{4,0},{1,5},{5,1},{2,6},{6,2},{3,7},{7,3},{8,12},{12,8},{9,1... | collective-permute-start | bytes 393224 | tf_op jit(solution)/shard_map/ppermute | solution.py:30
  75.4 1.3 %collective-permute-start.21 = (f32[256,128]{1,0:T(8,128)S(1)}, f32[256,128]{1,0:T(8,128)S(1)}, u32[]{:S(2)}, u32[]{:S(2)}) collective-permute-start(f32[256,128]{1,0:T(8,128)S(1)} %collective-permute-done.17.refs_3_), channel_id=1, source_target_pairs={{0,4},{4,0},{1,5},{5,1},{2,6},{6,2},{3,7},{7,3},{8,12},{12,8},{9,1... | collective-permute-start | bytes 393224 | tf_op jit(solution)/shard_map/ppermute | solution.py:30
  76.8 14.8 %copy-start.1 = (bf16[512,512]{1,0:T(8,128)(2,1)S(1)}, bf16[512,512]{1,0:T(8,128)(2,1)}, u32[]{:S(2)}) copy-start(bf16[512,512]{1,0:T(8,128)(2,1)} %get-tuple-element.44.low) | copy-start | bytes 1572868
  78.2 13.4 %copy-start = (bf16[512,512]{1,0:T(8,128)(2,1)S(1)}, bf16[512,512]{1,0:T(8,128)(2,1)}, u32[]{:S(2)}) copy-start(bf16[512,512]{1,0:T(8,128)(2,1)} %get-tuple-element.43.high) | copy-start | bytes 1572868
  78.2 6.8 %collective-permute-start.22 = (f32[8,32,128]{2,1,0:T(8,128)S(1)}, f32[8,32,128]{2,1,0:T(8,128)S(1)}, u32[]{:S(2)}, u32[]{:S(2)}) collective-permute-start(f32[8,32,128]{2,1,0:T(8,128)S(1)} %get-tuple-element.40), channel_id=1, source_target_pairs={{0,1},{1,2},{2,3},{3,0},{4,5},{5,6},{6,7},{7,4},{8,9},{9,10},{10,1... | collective-permute-start | bytes 393224 | tf_op jit(solution)/shard_map/ppermute | solution.py:30
  78.7 7.8 %collective-permute-start.23 = (f32[8,32,128]{2,1,0:T(8,128)S(1)}, f32[8,32,128]{2,1,0:T(8,128)S(1)}, u32[]{:S(2)}, u32[]{:S(2)}) collective-permute-start(f32[8,32,128]{2,1,0:T(8,128)S(1)} %get-tuple-element.41), channel_id=1, source_target_pairs={{0,2},{1,3},{2,0},{3,1},{4,6},{5,7},{6,4},{7,5},{8,10},{9,11},{10,... | collective-permute-start | bytes 393224 | tf_op jit(solution)/shard_map/ppermute | solution.py:30
  80.3 7.3 %collective-permute-start.24 = (f32[8,32,128]{2,1,0:T(8,128)S(1)}, f32[8,32,128]{2,1,0:T(8,128)S(1)}, u32[]{:S(2)}, u32[]{:S(2)}) collective-permute-start(f32[8,32,128]{2,1,0:T(8,128)S(1)} %get-tuple-element.42), channel_id=1, source_target_pairs={{0,3},{1,0},{2,1},{3,2},{4,7},{5,4},{6,5},{7,6},{8,11},{9,8},{10,9... | collective-permute-start | bytes 393224 | tf_op jit(solution)/shard_map/ppermute | solution.py:30
  88.2 11.3 %all-to-all-start.1 = ((f32[8,32,128]{2,1,0:T(8,128)}), f32[8,32,128]{2,1,0:T(8,128)S(1)}, u32[]{:S(2)}, u32[]{:S(2)}) async-start(f32[8,32,128]{2,1,0:T(8,128)} %shard_map.84), calls=%async_computation.1 | async-start | bytes 262144 | tf_op jit(solution)/shard_map/all_to_all | solution.py:306
